TPU v7x, 8 devices: a whole 2x2x1 slice. The times are simulated.
8 devices in a mesh: dp: 1 (over z), ty: 2 (over y), tx: 4 (over x, core).
Axes of the slice: x: 2, y: 2, z: 1, core: 2. Of those that a mesh axis runs over, the one named last changes fastest.
Arguments:
- x_in: bfloat16 [2, 128, 4096], P(('dp', 'ty'), None, 'tx')
- w_q: bfloat16 [4096, 4096], P('tx', 'ty')
- w_k: bfloat16 [4096, 4096], P('tx', 'ty')
- w_v: bfloat16 [4096, 4096], P('tx', 'ty')
- w_o: bfloat16 [4096, 4096], P('ty', 'tx')
- w_gate: bfloat16 [4096, 11008], P('tx', 'ty')
- w_up: bfloat16 [4096, 11008], P('tx', 'ty')
- w_down: bfloat16 [11008, 4096], P('ty', 'tx')
Outputs:
- output: bfloat16 [2, 128, 4096], P(('dp', 'ty'), None, 'tx')
All inputs are finite; a program needn't handle non-finite values.
Results may differ from a plain program's by a relative error of at most 0.02.
Values are sent between devices in bfloat16 or wider.
A program may use at most 1 GiB of HBM per device.

v0:
```python
import jax
import jax.numpy as jnp
from jax import lax
from jax.sharding import PartitionSpec as P, NamedSharding

HEAD_DIM = 128
EPS = 1e-5
THETA = 10000.0


def rotary(heads_bf):
    seq_len = heads_bf.shape[1]
    half_dim = HEAD_DIM // 2
    inv_freq = THETA ** (-2.0 * jnp.arange(half_dim, dtype=jnp.float32) / HEAD_DIM)
    angles = jnp.arange(seq_len, dtype=jnp.float32)[:, None] * inv_freq[None, :]
    cos_t = jnp.cos(angles)[:, None, :]
    sin_t = jnp.sin(angles)[:, None, :]
    values = heads_bf.astype(jnp.float32)
    lower_half = values[..., :half_dim]
    upper_half = values[..., half_dim:]
    return jnp.concatenate([lower_half * cos_t - upper_half * sin_t, upper_half * cos_t + lower_half * sin_t], axis=-1).astype(jnp.bfloat16)


def causal_attention(q_heads, k_heads, v_heads):
    seq_len = q_heads.shape[1]
    q_block = min(seq_len, 128)
    key_pos = jnp.arange(seq_len)
    scale_qk = HEAD_DIM ** -0.5

    def one_block(block_idx, out_acc):
        q_start = block_idx * q_block
        q_blk = lax.dynamic_slice_in_dim(q_heads, q_start, q_block, axis=1)
        scores = jnp.einsum("nqhd,nkhd->nhqk", q_blk, k_heads, preferred_element_type=jnp.float32) * scale_qk
        q_pos = q_start + jnp.arange(q_block)
        allowed = q_pos[:, None] >= key_pos[None, :]
        scores = jnp.where(allowed, scores, -1e30)
        prob_blk = jax.nn.softmax(scores, axis=-1).astype(jnp.bfloat16)
        blk_out = jnp.einsum("nhqk,nkhd->nqhd", prob_blk, v_heads, preferred_element_type=jnp.float32).astype(jnp.bfloat16)
        return lax.dynamic_update_slice_in_dim(out_acc, blk_out, q_start, axis=1)

    return lax.fori_loop(0, seq_len // q_block, one_block, jnp.zeros_like(q_heads))


def norm_sharded(values_bf, full_width):
    values = values_bf.astype(jnp.float32)
    moments = jnp.stack([jnp.sum(values, axis=-1), jnp.sum(values * values, axis=-1)], axis=-1)
    moments = lax.psum(moments, "tx")
    mean_val = moments[..., 0:1] / full_width
    var_val = moments[..., 1:2] / full_width - mean_val * mean_val
    return ((values - mean_val) * lax.rsqrt(var_val + EPS)).astype(jnp.bfloat16)


def project(rows_bf, weight):
    return jnp.einsum("...c,ch->...h", rows_bf, weight, preferred_element_type=jnp.float32).astype(jnp.bfloat16)


def solution(mesh):
    tx_count = mesh.shape["tx"]
    act_spec = P(("dp", "ty"), None, "tx")
    col_spec = P("tx", "ty")
    row_spec = P("ty", "tx")

    def layer_fn(x_blk, w_q, w_k, w_v, w_o, w_gate, w_up, w_down):
        full_width = x_blk.shape[-1] * tx_count
        normed_all = lax.all_gather(norm_sharded(x_blk, full_width), "ty", axis=0, tiled=True)
        q_sum, k_sum, v_sum = lax.psum((project(normed_all, w_q), project(normed_all, w_k), project(normed_all, w_v)), "tx")
        n_seqs, seq_len, local_cols = q_sum.shape
        head_shape = (n_seqs, seq_len, local_cols // HEAD_DIM, HEAD_DIM)
        attn_heads = causal_attention(rotary(q_sum.reshape(head_shape)), rotary(k_sum.reshape(head_shape)), v_sum.reshape(head_shape))
        attn_out = lax.psum_scatter(project(attn_heads.reshape(q_sum.shape), w_o), "ty", scatter_dimension=0, tiled=True)
        resid_h = (x_blk.astype(jnp.float32) + attn_out.astype(jnp.float32)).astype(jnp.bfloat16)
        normed_mlp = lax.all_gather(norm_sharded(resid_h, full_width), "ty", axis=0, tiled=True)
        gate_sum, up_sum = lax.psum((project(normed_mlp, w_gate), project(normed_mlp, w_up)), "tx")
        act_val = (jax.nn.silu(gate_sum.astype(jnp.float32)) * up_sum.astype(jnp.float32)).astype(jnp.bfloat16)
        mlp_out = lax.psum_scatter(project(act_val, w_down), "ty", scatter_dimension=0, tiled=True)
        return (resid_h.astype(jnp.float32) + mlp_out.astype(jnp.float32)).astype(jnp.bfloat16)

    return jax.shard_map(layer_fn, mesh=mesh, in_specs=(act_spec, col_spec, col_spec, col_spec, row_spec, col_spec, col_spec, row_spec), out_specs=act_spec, check_vma=False)
```

profile of v0, /device:TPU:0, one launch (start us, length us, event | category | flops | bytes accessed | tf_op | source)
XLA Modules:
  0.0 292.8 jit_solution(12989174328045026802)
XLA Ops:
  7.6 8.8 %psum.49 = f32[1,128,2]{1,2,0:T(2,128)S(1)} all-reduce(f32[1,128,2]{1,2,0:T(2,128)S(1)} %pad_maximum_fusion), channel_id=1, replica_groups=mesh['dp'=1,'ty'=2,'tx'=4] {'tx'}, use_global_device_ids=true, to_apply=%region_2.0 | all-reduce | flops 256 | bytes 2048 | tf_op jit(solution)/shard_map/psum | solution.py:47
  16.4 1.2 fusion.65
  17.6 7.4 %all_gather.6 = bf16[2,128,1024]{2,1,0:T(8,128)(2,1)S(1)} all-gather(bf16[1,128,1024]{2,1,0:T(8,128)(2,1)S(1)} %fusion.65), channel_id=1, replica_groups=mesh['dp'=1,'ty'=2,'tx'=4] {'ty'}, dimensions={0}, use_global_device_ids=true | all-gather | bytes 786432 | tf_op jit(solution)/shard_map/all_gather | solution.py:65
  25.0 3.6 %fusion.38 = bf16[2,16,16,8,128]{4,3,2,1,0:T(8,128)(2,1)S(1)} fusion(bf16[2,128,1024]{2,1,0:T(8,128)(2,1)S(1)} %all_gather.6, bf16[1024,2048]{1,0:T(8,128)(2,1)} %param.10), kind=kOutput, calls=%fused_computation.37 | convolution fusion | flops 1074266112 | bytes 5767168 | tf_op jit(solution)/shard_map/...c,ch->...h/dot_general | solution.py:54
  28.6 1.3 fusion.41
  30.8 1.3 fusion.28
  32.1 1.3 copy.21
  33.4 1.9 copy_bitcast_fusion
  35.7 63.7 %all-reduce.7.cloned.1.call-done = (bf16[2,128,16,128]{1,3,2,0:T(8,128)(2,1)}, bf16[2,128,16,128]{3,1,2,0:T(8,128)(2,1)}, bf16[2,128,16,128]{3,1,2,0:T(8,128)(2,1)}) async-done(((bf16[2,128,16,128]{1,3,2,0:T(8,128)(2,1)}, bf16[2,128,16,128]{3,1,2,0:T(8,128)(2,1)}, bf16[2,128,16,128]{3,1,2,0:T(8,128)(2,1)}), (bf16[2,128,16,128]{1,3,2,0:T(8,128)(2,1)}, bf16[2,128,16,128]{3,1,2,0:T(8,128)(2,1)}, ...) | async-done | bytes 3145744 | tf_op jit(solution)/shard_map/psum | solution.py:66
  99.4 1.5 convert_element_type.86
  101.2 2.5 subtract_convert_fusion
  103.7 4.2 %fusion.94 = (f32[2,16,128]{2,1,0:T(8,128)S(1)}, f32[2,16,128,128]{2,3,1,0:T(8,128)}) fusion(pred[128,128]{0,1:T(8,128)(4,1)S(1)} %iota_compare_fusion, bf16[2,128,16,64]{3,1,2,0:T(8,128)(2,1)S(1)} %get-tuple-element.37, bf16[2,128,16,64]{3,1,2,0:T(8,128)(2,1)S(1)} %get-tuple-element.36, bf16[2,128,16,64]{3,1,2,0:T(8,128)(2,1)S(1)} %get-tuple-element.40, ...), kind=kOutput, calls=%fused_computation.88 | convolution fusion | flops 140509312 | bytes 4227072 | tf_op jit(solution)/shard_map/while/body/eval_jaxpr/sub | solution.py:37
  107.9 2.5 convolution_convert_fusion
  111.1 2.1 fusion.44
  113.2 12.0 %reduce-scatter.3.cloned.1.call-done = bf16[1,128,1024]{2,1,0:T(8,128)(2,1)} async-done(((bf16[2,128,1024]{2,1,0:T(8,128)(2,1)}), bf16[1,128,1024]{2,1,0:T(8,128)(2,1)}) %reduce-scatter.3.cloned.1.call-update) | async-done | bytes 262160 | tf_op jit(solution)/shard_map/reduce_scatter | solution.py:70
  125.2 1.1 convert_reduce_fusion
  126.3 6.3 %psum.53 = f32[1,128,2]{1,2,0:T(2,128)S(1)} all-reduce(f32[1,128,2]{1,2,0:T(2,128)S(1)} %pad_maximum_fusion.1), channel_id=1, replica_groups=mesh['dp'=1,'ty'=2,'tx'=4] {'tx'}, use_global_device_ids=true, to_apply=%region_11.12 | all-reduce | flops 256 | bytes 2048 | tf_op jit(solution)/shard_map/psum | solution.py:47
  132.9 8.3 %all_gather.7 = bf16[2,128,1024]{2,1,0:T(8,128)(2,1)S(1)} all-gather(bf16[1,128,1024]{2,1,0:T(8,128)(2,1)S(1)} %fusion.69), channel_id=1, replica_groups=mesh['dp'=1,'ty'=2,'tx'=4] {'ty'}, dimensions={0}, use_global_device_ids=true | all-gather | bytes 786432 | tf_op jit(solution)/shard_map/all_gather | solution.py:72
  141.2 8.8 %fusion.10 = bf16[2,128,5504]{2,1,0:T(8,128)(2,1)} fusion(bf16[2,128,1024]{2,1,0:T(8,128)(2,1)S(1)} %all_gather.7, bf16[1024,5504]{1,0:T(8,128)(2,1)} %param.14), kind=kOutput, calls=%fused_computation.8 | convolution fusion | flops 2887090176 | bytes 14614528 | tf_op jit(solution)/shard_map/...c,ch->...h/dot_general | solution.py:54
  149.9 8.8 %fusion.7 = bf16[2,128,5504]{2,1,0:T(8,128)(2,1)} fusion(bf16[2,128,1024]{2,1,0:T(8,128)(2,1)S(1)} %all_gather.7, bf16[1024,5504]{1,0:T(8,128)(2,1)} %param.13), kind=kOutput, calls=%fused_computation.7 | convolution fusion | flops 2887090176 | bytes 14614528 | tf_op jit(solution)/shard_map/...c,ch->...h/dot_general | solution.py:54
  158.7 103.3 %all-reduce.5.cloned.1.call-done = (bf16[2,128,5504]{2,1,0:T(8,128)(2,1)}, bf16[2,128,5504]{2,1,0:T(8,128)(2,1)}) async-done(((bf16[2,128,5504]{2,1,0:T(8,128)(2,1)}, bf16[2,128,5504]{2,1,0:T(8,128)(2,1)}), (bf16[2,128,5504]{2,1,0:T(8,128)(2,1)}, bf16[2,128,5504]{2,1,0:T(8,128)(2,1)})) %all-reduce.5.cloned.1.call-update) | async-done | bytes 5636112 | tf_op jit(solution)/shard_map/psum | solution.py:73
  262.1 10.4 %fusion.47 = bf16[2,128,1024]{2,1,0:T(8,128)(2,1)} fusion(bf16[5504,1024]{1,0:T(8,128)(2,1)} %param.15, bf16[2,128,5504]{2,1,0:T(8,128)(2,1)} %get-tuple-element.28, bf16[2,128,5504]{2,1,0:T(8,128)(2,1)} %get-tuple-element.30), kind=kOutput, calls=%fused_computation.40 | convolution fusion | flops 2897215488 | bytes 17432576 | tf_op jit(solution)/shard_map/...c,ch->...h/dot_general | solution.py:54
  272.4 12.1 %reduce-scatter.5.cloned.1.call-done = bf16[1,128,1024]{2,1,0:T(8,128)(2,1)} async-done(((bf16[2,128,1024]{2,1,0:T(8,128)(2,1)}), bf16[1,128,1024]{2,1,0:T(8,128)(2,1)}) %reduce-scatter.5.cloned.1.call-update) | async-done | bytes 262160 | tf_op jit(solution)/shard_map/reduce_scatter | solution.py:75
  284.6 1.7 fusion.70
  (28 shorter events, 3.6 us)
Async XLA Ops:
  6.5 92.9 %all-reduce.7.cloned.1.call-start = ((), (), s32[]{:S(2)}) async-start(), calls=%async_computation.5 | async-start | bytes 6291456 | tf_op jit(solution)/shard_map/psum | solution.py:66
  25.0 3.6 %copy-start.3 = (bf16[1024,2048]{1,0:T(8,128)(2,1)S(1)}, bf16[1024,2048]{1,0:T(8,128)(2,1)}, u32[]{:S(2)}) copy-start(bf16[1024,2048]{1,0:T(8,128)(2,1)} %param.9) | copy-start | bytes 12582916
  28.6 2.2 copy-start.4
  35.3 89.8 %reduce-scatter.3.cloned.1.call-start = ((), (), s32[]{:S(2)}) async-start(), calls=%async_computation.2 | async-start | bytes 786432 | tf_op jit(solution)/shard_map/reduce_scatter | solution.py:70
  99.4 1.6 copy-start.2
  107.9 3.1 %copy-start = (bf16[2048,1024]{1,0:T(8,128)(2,1)S(1)}, bf16[2048,1024]{1,0:T(8,128)(2,1)}, u32[]{:S(2)}) copy-start(bf16[2048,1024]{1,0:T(8,128)(2,1)} %param.12) | copy-start | bytes 12582916
  111.1 14.1 %copy-start.1 = (bf16[1,128,1024]{2,1,0:T(8,128)(2,1)S(1)}, bf16[1,128,1024]{2,1,0:T(8,128)(2,1)}, u32[]{:S(2)}) copy-start(bf16[1,128,1024]{2,1,0:T(8,128)(2,1)} %param.8) | copy-start | bytes 786436
  113.2 148.9 %all-reduce.5.cloned.1.call-start = ((), (), s32[]{:S(2)}) async-start(), calls=%async_computation.4 | async-start | bytes 11272192 | tf_op jit(solution)/shard_map/psum | solution.py:73
  158.7 125.9 %reduce-scatter.5.cloned.1.call-start = ((), (), s32[]{:S(2)}) async-start(), calls=%async_computation.3 | async-start | bytes 786432 | tf_op jit(solution)/shard_map/reduce_scatter | solution.py:75
Sparse Core Ops, SparseCore 0:
  35.5 63.9 all-reduce.6
  113.3 11.8 reduce-scatter.2
  158.8 103.1 all-reduce.4
  272.6 11.9 reduce-scatter.4
where the time goes:
time: 293 us
  waiting for transfers between devices  191 us (65%)
  matrix products  42.8 us (15%)
  blocking collectives  30.7 us (10%)
  between operations  13.2 us (5%)
  other arithmetic  9.92 us (3%)
  local copies, waits for them, and re-layouts  4.79 us (2%)
    psum x1, waiting for transfers between devices, layer_fn(): lax.psum((project(normed_mlp, w_gate), project(normed_mlp, w_up)), 'tx')  103 us
    psum x1, waiting for transfers between devices, layer_fn(): lax.psum((project(normed_all, w_q), project(normed_all, w_k), project(nor...  63.7 us
    dot_general x7, matrix products, project(): jnp.einsum('...c,ch->...h', rows_bf, weight, preferred_element_type=jnp.f...  36.1 us
    psum x2, blocking collectives, norm_sharded(): moments = lax.psum(moments, 'tx')  15.1 us
    reduce_scatter x1, waiting for transfers between devices, layer_fn(): lax.psum_scatter(project(act_val, w_down), 'ty', scatter_dimension=0, til...  12.1 us
    reduce_scatter x1, waiting for transfers between devices, layer_fn(): lax.psum_scatter(project(attn_heads.reshape(q_sum.shape), w_o), 'ty', sca...  12 us
    all_gather x1, blocking collectives, layer_fn(): lax.all_gather(norm_sharded(resid_h, full_width), 'ty', axis=0, tiled=True)  8.28 us
    all_gather x1, blocking collectives, layer_fn(): lax.all_gather(norm_sharded(x_blk, full_width), 'ty', axis=0, tiled=True)  7.38 us
  transfers between devices with their start and end apart: 4, of which 4 were waited for; matrix products, arithmetic and copies ran while one was open for 0% of the time, Pallas kernels for 0%

commit v1 on v0

v1 whole, which is shorter than its diff:
```python
import numpy as np

import jax
import jax.numpy as jnp
from jax import lax
from jax.experimental import pallas as pl
from jax.experimental.pallas import tpu as pltpu
from jax.sharding import PartitionSpec as P

HEAD_DIM = 128
EPS = 1e-5
THETA = 10000.0
BF = jnp.bfloat16
F32 = jnp.float32
MESH = pl.DeviceIdType.MESH

HALF = 64
ROWS = 128
SUB = 32
FW = 1024


def dot(a, b):
    return jnp.dot(a, b, preferred_element_type=F32)


def dot_t(a, b):
    return lax.dot_general(a, b, (((1,), (1,)), ((), ())), preferred_element_type=F32)


def rotary_tables(seq_len):
    half_dim = HEAD_DIM // 2
    inv_freq = (np.float32(THETA) ** (np.float32(-2.0) * np.arange(half_dim, dtype=np.float32) / np.float32(HEAD_DIM))).astype(np.float32)
    angles = np.arange(seq_len, dtype=np.float32)[:, None] * inv_freq[None, :]
    cos_t = np.cos(angles.astype(np.float64)).astype(np.float32)
    sin_t = np.sin(angles.astype(np.float64)).astype(np.float32)
    return np.concatenate([cos_t, cos_t], 1), np.concatenate([-sin_t, sin_t], 1)


def layer_kernel(x_hbm, wq_hbm, wk_hbm, wv_hbm, wo_hbm, wg_hbm, wu_hbm, wd_hbm, cos_hbm, sin_hbm, out_hbm,
                 wbuf, wo_v, wg_v, wu_v, cos_v, sin_v, x_all, n_buf, d_send, d_recv, x_recv, k_buf, v_buf, o_all,
                 p_send, p_recv, h_buf, g_send, g_recv, g_own, gx_recv, a_all, acc, f_send, f_recv, y_buf, st1, st2,
                 ld_sem, w_sem, xy_s, xy_r, s1_s, s1_r, d_s, d_r, x_s, x_r, o_s, o_r, p_s, p_r, s2_s, s2_r,
                 g_s, g_r, gx_s, gx_r, a_s, a_r, f_s, f_r):
    dp = lax.axis_index("dp")
    y = lax.axis_index("ty")
    t = lax.axis_index("tx")
    xc = lax.div(t, 2)
    c = lax.rem(t, 2)
    width = x_hbm.shape[2]
    cols = wq_hbm.shape[1] // 4
    ff = wg_hbm.shape[1]
    n_full = ff // FW
    last_w = ff - n_full * FW
    full_width = 4 * width
    rel = [t, t + 1 - 2 * c, t + 2 - 4 * xc, 3 - t]
    peer = [(dp, y, r) for r in rel]
    other = [(dp, 1 - y, r) for r in rel]
    core_peer, x_peer, y_peer = peer[1], peer[2], other[0]

    def remote(src, dst, ss, rs, dev):
        return pltpu.make_async_remote_copy(src_ref=src, dst_ref=dst, send_sem=ss, recv_sem=rs, device_id=dev, device_id_type=MESH)

    def x_load(h):
        return pltpu.make_async_copy(x_hbm.at[0, pl.ds(h * HALF, HALF)], x_all.at[h, y], ld_sem.at[h])

    tables = [pltpu.make_async_copy(cos_hbm, cos_v, ld_sem.at[2]), pltpu.make_async_copy(sin_hbm, sin_v, ld_sem.at[3])]

    def qkv_load(r, m):
        src = (wq_hbm, wk_hbm, wv_hbm)[m].at[:, pl.ds(pl.multiple_of(rel[r] * cols, cols), cols)]
        return pltpu.make_async_copy(src, wbuf.at[r * 3 + m], w_sem.at[r * 3 + m])

    def qkv_wait(r, m):
        pltpu.make_async_copy(wq_hbm.at[:, pl.ds(0, cols)], wbuf.at[r * 3 + m], w_sem.at[r * 3 + m]).wait()

    wo_load = pltpu.make_async_copy(wo_hbm, wo_v, w_sem.at[12])

    def gu_load(i, j, w):
        src, dst = ((wg_hbm, wg_v), (wu_hbm, wu_v))[i]
        start = j * FW if isinstance(j, int) else pl.multiple_of(j * FW, FW)
        return pltpu.make_async_copy(src.at[:, pl.ds(start, w)], dst.at[:, pl.ds(start, w)], w_sem.at[16 + i * 8 + j])

    def down_load(j, nh, w):
        start = j * FW if isinstance(j, int) else pl.multiple_of(j * FW, FW)
        return pltpu.make_async_copy(wd_hbm.at[pl.ds(start, w), pl.ds(nh * 512, 512)], wbuf.at[j * 2 + nh, pl.ds(0, w)], w_sem.at[32 + j * 2 + nh])

    def xy_copy(h):
        return remote(x_all.at[h, y], x_all.at[h, y], xy_s.at[h], xy_r.at[h], y_peer)

    def s1_copy(k):
        return remote(st1.at[0], st1.at[k], s1_s.at[k], s1_r.at[k], peer[k] if k < 4 else other[k - 4])

    def d_copy(h, z, m):
        i = (h * 2 + z) * 3 + m
        return remote(d_send.at[i], d_recv.at[i], d_s.at[i], d_r.at[i], core_peer)

    def x_copy(h, m):
        i = h * 3 + m
        return remote(d_recv.at[h * 6 + m], x_recv.at[i], x_s.at[i], x_r.at[i], x_peer)

    def o_copy(h, kind):
        slot = (t, t, rel[2])[kind]
        i = h * 3 + kind
        return remote(o_all.at[h, slot], o_all.at[h, slot], o_s.at[i], o_r.at[i], (core_peer, x_peer, core_peer)[kind])

    def p_copy(h):
        return remote(p_send.at[h], p_recv.at[h], p_s.at[h], p_r.at[h], y_peer)

    def s2_copy(h, k):
        i = h * 4 + k
        return remote(st2.at[h, 0], st2.at[h, k], s2_s.at[i], s2_r.at[i], peer[k])

    def g_copy(h, j, w):
        i = h * 6 + j
        return remote(g_send.at[i, :, :, pl.ds(0, w)], g_recv.at[i, :, :, pl.ds(0, w)], g_s.at[i], g_r.at[i], core_peer)

    def gx_copy(h, j, w):
        i = h * 6 + j
        return remote(g_recv.at[i, :, pl.ds(0, SUB), pl.ds(0, w)], gx_recv.at[i, :, :, pl.ds(0, w)], gx_s.at[i], gx_r.at[i], x_peer)

    def a_copy(h, j, w, kind):
        own = c * 2 + xc
        slot = (own, own, c * 2 + 1 - xc)[kind]
        i = h * 6 + j
        ref = a_all.at[i, slot, :, pl.ds(0, w)]
        return remote(ref, ref, a_s.at[i * 3 + kind], a_r.at[i * 3 + kind], (core_peer, x_peer, core_peer)[kind])

    def f_copy(h):
        return remote(f_send.at[h], f_recv.at[h], f_s.at[h], f_r.at[h], y_peer)

    lane = lax.broadcasted_iota(jnp.int32, (128, 128), 1)
    sublane = lax.broadcasted_iota(jnp.int32, (128, 128), 0)

    def local_stats(v):
        s = jnp.sum(v, axis=1, keepdims=True)
        q = jnp.sum(v * v, axis=1, keepdims=True)
        m = jnp.where(lane == 0, s, jnp.where(lane == 1, q, 0.0))
        return m.T[0:8]

    def moments(total):
        mean = total[0:1] / full_width
        var = total[1:2] / full_width - mean * mean
        rstd = lax.rsqrt(var + EPS)
        m = jnp.where(sublane == 0, mean, jnp.where(sublane == 1, rstd, 0.0)).T
        return m[:, 0:1], m[:, 1:2]

    def x_own(h, s):
        return x_all[h, s].astype(F32)

    for h in range(2):
        x_load(h).start()
    for r in (3, 2, 1, 0):
        for m in range(3):
            qkv_load(r, m).start()
    for tb in tables:
        tb.start()
    barrier = pltpu.get_barrier_semaphore()
    for dev in peer[1:] + other:
        pl.semaphore_signal(barrier, inc=1, device_id=dev, device_id_type=MESH)
    for h in range(2):
        x_load(h).wait()
    st1[0] = local_stats(jnp.concatenate([x_own(0, y), x_own(1, y)], axis=0))
    pl.semaphore_wait(barrier, 7)
    for k in range(1, 8):
        s1_copy(k).start()
    for h in range(2):
        xy_copy(h).start()
    wo_load.start()
    for k in range(1, 4):
        s1_copy(k).wait_recv()
    mean_o, rstd_o = moments((st1[0] + st1[1]) + (st1[2] + st1[3]))
    for k in range(4, 8):
        s1_copy(k).wait_recv()
    mean_p, rstd_p = moments((st1[4] + st1[5]) + (st1[6] + st1[7]))

    def norm_rows(h, s, mean, rstd):
        sl = slice(h * HALF, (h + 1) * HALF)
        n = ((x_own(h, s) - mean[sl]) * rstd[sl]).astype(BF)
        n_buf[h, pl.ds(pl.multiple_of(s * HALF, HALF), HALF)] = n

    def qkv_block(h, r, after):
        def body(m, carry):
            if h == 0:
                qkv_wait(r, m)
            after(m, dot(n_buf[h], wbuf[r * 3 + m]))
            return carry

        lax.fori_loop(0, 3, body, 0)

    def qkv_send(h):
        def give(z):
            def after(m, res):
                d_send[(h * 2 + z) * 3 + m] = res.astype(BF)
                d_copy(h, z, m).start()
            return after

        def take(z):
            def after(m, res):
                d_copy(h, z, m).wait_recv()
                i = (h * 2 + z) * 3 + m
                d_recv[i] = (res + d_recv[i].astype(F32)).astype(BF)
                if z == 0:
                    x_copy(h, m).start()
            return after

        qkv_block(h, 3, give(0))
        qkv_block(h, 2, take(0))
        qkv_block(h, 1, give(1))
        qkv_block(h, 0, take(1))

    def rotate(v, cos2, sin2):
        f = v.astype(F32)
        return (f * cos2 + pltpu.roll(f, HEAD_DIM // 2, 1) * sin2).astype(BF)

    def attention(h):
        for m in range(3):
            x_copy(h, m).wait_recv()

        def final(m):
            return (d_recv[h * 6 + 3 + m].astype(F32) + x_recv[h * 3 + m].astype(F32)).astype(BF)

        sl = slice(h * HALF, (h + 1) * HALF)
        n_keys = (h + 1) * HALF
        cos2 = jnp.concatenate([cos_v[sl], cos_v[sl]], axis=0)
        sin2 = jnp.concatenate([sin_v[sl], sin_v[sl]], axis=0)
        q, k, v = final(0), final(1), final(2)
        for s in range(2):
            v_buf[s, sl] = v[s * HALF:(s + 1) * HALF]
        q_pos = h * HALF + lax.broadcasted_iota(jnp.int32, (HALF, n_keys), 0)
        k_pos = lax.broadcasted_iota(jnp.int32, (HALF, n_keys), 1)
        allowed = q_pos >= k_pos
        for hd in range(cols // HEAD_DIM):
            cl = slice(hd * HEAD_DIM, (hd + 1) * HEAD_DIM)
            qr = rotate(q[:, cl], cos2, sin2)
            kr = rotate(k[:, cl], cos2, sin2)
            for s in range(2):
                rs = slice(s * HALF, (s + 1) * HALF)
                k_buf[s, sl, cl] = kr[rs]
                keys = kr[rs] if h == 0 else jnp.concatenate([k_buf[s, 0:HALF, cl], kr[rs]], axis=0)
                vals = v[rs, cl] if h == 0 else jnp.concatenate([v_buf[s, 0:HALF, cl], v[rs, cl]], axis=0)
                scores = dot_t(qr[rs], keys) * (HEAD_DIM ** -0.5)
                scores = jnp.where(allowed, scores, -1e30)
                e = jnp.exp(scores - jnp.max(scores, axis=1, keepdims=True))
                prob = (e / jnp.sum(e, axis=1, keepdims=True)).astype(BF)
                o_all[h, t, rs, cl] = dot(prob, vals).astype(BF)
        o_copy(h, 1).start()
        o_copy(h, 0).start()

    def relay_o(h):
        o_copy(h, 1).wait_recv()
        o_copy(h, 2).start()

    def project_o(h):
        o_copy(h, 0).wait_recv()
        o_copy(h, 2).wait_recv()
        for nh in range(2):
            cl = slice(nh * 512, (nh + 1) * 512)
            res = jnp.zeros((ROWS, 512), F32)
            for b in range(4):
                res = res + dot(o_all[h, b], wo_v[b * cols:(b + 1) * cols, cl])
            p_send[h, :, cl] = res.astype(BF)
        p_copy(h).start()

    def residual(h):
        p_copy(h).wait_recv()
        attn = (p_send[h].astype(F32) + p_recv[h].astype(F32)).astype(BF).astype(F32)
        xv = jnp.concatenate([x_own(h, 0), x_own(h, 1)], axis=0)
        hv = (xv + attn).astype(BF)
        h_buf[h] = hv
        st2[h, 0] = local_stats(hv.astype(F32))
        for k in range(1, 4):
            s2_copy(h, k).start()

    def norm2(h):
        for k in range(1, 4):
            s2_copy(h, k).wait_recv()
        mean, rstd = moments((st2[h, 0] + st2[h, 1]) + (st2[h, 2] + st2[h, 3]))
        n = ((h_buf[h].astype(F32) - mean) * rstd).astype(BF)
        for b in range(4):
            e_c = c if b // 2 == 1 else 1 - c
            e_x = xc if b % 2 == 1 else 1 - xc
            n_buf[h, pl.ds(pl.multiple_of(64 * e_c + 32 * e_x, SUB), SUB)] = n[b * SUB:(b + 1) * SUB]

    def gu_mul(h, j, w):
        slot = lax.rem(j, 2)
        for i, wv in enumerate((wg_v, wu_v)):
            if h == 0:
                gu_load(i, j, w).wait()
            for n0 in range(0, w, 512):
                nw = min(512, w - n0)
                start = j * FW + n0 if isinstance(j, int) else pl.multiple_of(j * FW + n0, 512)
                res = dot(n_buf[h], wv[:, pl.ds(start, nw)])
                g_send[h * 6 + j, i, :, n0:n0 + nw] = res[0:64].astype(BF)
                g_own[slot, i, :, n0:n0 + nw] = res[64:128]
        g_copy(h, j, w).start()

    def gu_add(h, j, w):
        slot = lax.rem(j, 2)
        g_copy(h, j, w).wait_recv()
        i = h * 6 + j
        for k in range(2):
            g_recv[i, k, :, 0:w] = (g_own[slot, k, :, 0:w] + g_recv[i, k, :, 0:w].astype(F32)).astype(BF)
        gx_copy(h, j, w).start()

    def gate_up(h):
        gu_mul(h, 0, FW)

        def body(j, carry):
            gu_mul(h, j, FW)
            gu_add(h, j - 1, FW)
            return carry

        lax.fori_loop(1, n_full, body, 0)
        gu_mul(h, n_full, last_w)
        gu_add(h, n_full - 1, FW)
        gu_add(h, n_full, last_w)

    def act(h, j, w):
        gx_copy(h, j, w).wait_recv()
        i = h * 6 + j
        g, u = [
            (g_recv[i, k, SUB:2 * SUB, 0:w].astype(F32) + gx_recv[i, k, :, 0:w].astype(F32)).astype(BF).astype(F32)
            for k in range(2)
        ]
        a_all[i, c * 2 + xc, :, 0:w] = (g * (1.0 / (1.0 + jnp.exp(-g))) * u).astype(BF)
        a_copy(h, j, w, 1).start()
        a_copy(h, j, w, 0).start()

    def relay_a(h, j, w):
        a_copy(h, j, w, 1).wait_recv()
        a_copy(h, j, w, 2).start()

    def down(h, j, w):
        a_copy(h, j, w, 0).wait_recv()
        a_copy(h, j, w, 2).wait_recv()
        lhs = a_all[h * 6 + j, :, :, 0:w].reshape(ROWS, w)
        for nh in range(2):
            if h == 0:
                down_load(j, nh, w).wait()
            acc[h, :, nh * 512:(nh + 1) * 512] += dot(lhs, wbuf[j * 2 + nh, 0:w])

    def mlp_out(h):
        acc[h] = jnp.zeros((ROWS, width), F32)
        act(h, 0, FW)
        act(h, 1, FW)
        relay_a(h, 0, FW)

        def body(j, carry):
            act(h, j, FW)
            relay_a(h, j - 1, FW)
            down(h, j - 2, FW)
            return carry

        lax.fori_loop(2, n_full, body, 0)
        act(h, n_full, last_w)
        relay_a(h, n_full - 1, FW)
        down(h, n_full - 2, FW)
        relay_a(h, n_full, last_w)
        down(h, n_full - 1, FW)
        down(h, n_full, last_w)
        f_send[h] = acc[h, pl.ds(pl.multiple_of((1 - y) * HALF, HALF), HALF)].astype(BF)
        f_copy(h).start()

    def store_out(h):
        own = pl.ds(pl.multiple_of(y * HALF, HALF), HALF)
        f_copy(h).wait_recv()
        mlp = (acc[h, own].astype(BF).astype(F32) + f_recv[h].astype(F32)).astype(BF).astype(F32)
        y_buf[h] = (h_buf[h, own].astype(F32) + mlp).astype(BF)
        return pltpu.make_async_copy(y_buf.at[h], out_hbm.at[0, pl.ds(h * HALF, HALF)], ld_sem.at[h])

    norm_rows(0, y, mean_o, rstd_o)
    xy_copy(0).wait_recv()
    norm_rows(0, 1 - y, mean_p, rstd_p)
    qkv_send(0)
    for j in range(n_full + 1):
        for i in range(2):
            gu_load(i, j, FW if j < n_full else last_w).start()
    norm_rows(1, y, mean_o, rstd_o)
    xy_copy(1).wait_recv()
    norm_rows(1, 1 - y, mean_p, rstd_p)
    qkv_send(1)
    for j in range(n_full + 1):
        for nh in range(2):
            down_load(j, nh, FW if j < n_full else last_w).start()
    for tb in tables:
        tb.wait()
    attention(0)
    wo_load.wait()
    relay_o(0)
    project_o(0)
    attention(1)
    residual(0)
    relay_o(1)
    project_o(1)
    norm2(0)
    gate_up(0)
    residual(1)
    norm2(1)
    gate_up(1)
    mlp_out(0)
    mlp_out(1)
    stores = []
    for h in range(2):
        cp = store_out(h)
        cp.start()
        stores.append(cp)

    for k in range(1, 8):
        s1_copy(k).wait_send()
    for h in range(2):
        xy_copy(h).wait_send()
        for m in range(3):
            d_copy(h, 0, m).wait_send()
            d_copy(h, 1, m).wait_send()
            x_copy(h, m).wait_send()
            o_copy(h, m).wait_send()
            s2_copy(h, m + 1).wait_send()
        p_copy(h).wait_send()
        for j in range(n_full + 1):
            w = FW if j < n_full else last_w
            g_copy(h, j, w).wait_send()
            gx_copy(h, j, w).wait_send()
            for kind in range(3):
                a_copy(h, j, w, kind).wait_send()
        f_copy(h).wait_send()
    for cp in stores:
        cp.wait()


def solution(mesh):
    act_spec = P(("dp", "ty"), None, "tx")
    col_spec = P("tx", "ty")
    row_spec = P("ty", "tx")

    def layer_fn(x_blk, w_q, w_k, w_v, w_o, w_gate, w_up, w_down):
        seq_len, width = x_blk.shape[1:]
        cols = w_q.shape[1] // 4
        ff = w_gate.shape[1]
        cos_t, sin_t = (jnp.asarray(a) for a in rotary_tables(seq_len))
        dma = pltpu.SemaphoreType.DMA
        vm = pltpu.VMEM
        return pl.pallas_call(
            layer_kernel,
            out_shape=jax.ShapeDtypeStruct(x_blk.shape, BF),
            in_specs=[pl.BlockSpec(memory_space=pl.ANY)] * 10,
            out_specs=pl.BlockSpec(memory_space=pl.ANY),
            scratch_shapes=[
                vm((12, width, cols), BF),
                vm(w_o.shape, BF),
                vm(w_gate.shape, BF),
                vm(w_up.shape, BF),
                vm((seq_len, HEAD_DIM), F32),
                vm((seq_len, HEAD_DIM), F32),
                vm((2, 2, HALF, width), BF),
                vm((2, ROWS, width), BF),
                vm((12, ROWS, cols), BF),
                vm((12, ROWS, cols), BF),
                vm((6, ROWS, cols), BF),
                vm((2, seq_len, cols), BF),
                vm((2, seq_len, cols), BF),
                vm((2, 4, ROWS, cols), BF),
                vm((2, ROWS, width), BF),
                vm((2, ROWS, width), BF),
                vm((2, ROWS, width), BF),
                vm((12, 2, 2 * SUB, FW), BF),
                vm((12, 2, 2 * SUB, FW), BF),
                vm((2, 2, 2 * SUB, FW), F32),
                vm((12, 2, SUB, FW), BF),
                vm((12, 4, SUB, FW), BF),
                vm((2, ROWS, width), F32),
                vm((2, HALF, width), BF),
                vm((2, HALF, width), BF),
                vm((2, HALF, width), BF),
                vm((8, 8, 128), F32),
                vm((2, 4, 8, 128), F32),
                dma((4,)), dma((48,)),
                dma((2,)), dma((2,)), dma((8,)), dma((8,)), dma((12,)), dma((12,)), dma((6,)), dma((6,)),
                dma((6,)), dma((6,)), dma((2,)), dma((2,)), dma((8,)), dma((8,)), dma((12,)), dma((12,)),
                dma((12,)), dma((12,)), dma((36,)), dma((36,)), dma((2,)), dma((2,)),
            ],
            compiler_params=pltpu.CompilerParams(collective_id=0, has_side_effects=True, vmem_limit_bytes=67043328),
            name="layer",
        )(x_blk, w_q, w_k, w_v, w_o, w_gate, w_up, w_down, cos_t, sin_t)

    return jax.shard_map(layer_fn, mesh=mesh, in_specs=(act_spec, col_spec, col_spec, col_spec, row_spec, col_spec, col_spec, row_spec), out_specs=act_spec, check_vma=False)
```

time: 293 us -> 123 us (0.42)
  waiting for transfers between devices: 191 us -> 0 us
  Pallas kernels: 0 us -> 121 us
  matrix products: 42.8 us -> 0 us
  blocking collectives: 30.7 us -> 0 us
  between operations: 13.2 us -> 0.01 us
  other arithmetic: 9.92 us -> 0 us
  local copies, waits for them, and re-layouts: 4.79 us -> 1.67 us
    psum x2 -> x0, waiting for transfers between devices: 167 us -> none  [the longest x1 103 us: layer_fn(): lax.psum((project(normed_mlp, w_gate), project(normed_mlp, w_up)), 'tx')]
    pallas_call x0 -> x1, Pallas kernels: none -> 121 us  [layer_fn(): pl.pallas_call(layer_kernel, out_shape=jax.ShapeDtypeStruct(x_blk.shape,...]
    dot_general x8 -> x0, matrix products: 38.6 us -> none  [the longest x7 36.1 us: project(): jnp.einsum('...c,ch->...h', rows_bf, weight, preferred_element_type=jnp.f...]
    reduce_scatter x2 -> x0, waiting for transfers between devices: 24.1 us -> none  [the longest x1 12.1 us: layer_fn(): lax.psum_scatter(project(act_val, w_down), 'ty', scatter_dimension=0, til...]
    all_gather x2 -> x0, blocking collectives: 15.7 us -> none  [the longest x1 8.28 us: layer_fn(): lax.all_gather(norm_sharded(resid_h, full_width), 'ty', axis=0, tiled=True)]
    psum x2 -> x0, blocking collectives: 15.1 us -> none  [norm_sharded(): moments = lax.psum(moments, 'tx')]
    convert_element_type x5 -> x0, other arithmetic: 4.87 us -> none  [the longest x2 1.78 us: rotary(): values = heads_bf.astype(jnp.float32)]
    sub x1 -> x0, matrix products: 4.23 us -> none  [one_block(): prob_blk = jax.nn.softmax(scores, axis=-1).astype(jnp.bfloat16)]
  transfers between devices with their start and end apart: 4 -> 0, of which waited for: 4 -> 0; matrix products, arithmetic and copies ran while one was open for 0% -> 0% of each run, Pallas kernels for 0% -> 0%
where the time goes in v1:
time: 123 us
  Pallas kernels  121 us (98%)
  local copies, waits for them, and re-layouts  1.67 us (1%)
    pallas_call x1, Pallas kernels, layer_fn(): pl.pallas_call(layer_kernel, out_shape=jax.ShapeDtypeStruct(x_blk.shape,...  121 us

profile of v1, /device:TPU:0, one launch (start us, length us, event | category | flops | bytes accessed | tf_op | source)
XLA Modules:
  0.0 122.5 jit_solution(15017321437458829113)
XLA Ops:
  0.0 120.8 %layer.1 = bf16[1,128,1024]{2,1,0:T(8,128)(2,1)} custom-call(bf16[1,128,1024]{2,1,0:T(8,128)(2,1)} %x_hbm.1, bf16[1024,2048]{1,0:T(8,128)(2,1)} %wq_hbm.1, bf16[1024,2048]{1,0:T(8,128)(2,1)} %wk_hbm.1, bf16[1024,2048]{1,0:T(8,128)(2,1)} %wv_hbm.1, bf16[2048,1024]{1,0:T(8,128)(2,1)} %wo_hbm.1, bf16[1024,5504]{1,0:T(8,128)(2,1)} %wg_hbm.1, ...), custom_call_target="tpu_custom_call" | custom-call | tf_op jit(solution)/shard_map/layer/pallas_call | solution.py:442
  120.8 1.7 %copy.12 = bf16[1,128,1024]{2,1,0:T(8,128)(2,1)} copy(bf16[1,128,1024]{2,1,0:T(8,128)(2,1)} %layer.1) | data formatting | bytes 524288

commit v2 on v1

--- a/solution.py
+++ b/solution.py
@@ -90,21 +90,33 @@
     def s1_copy(k):
         return remote(st1.at[0], st1.at[k], s1_s.at[k], s1_r.at[k], peer[k] if k < 4 else other[k - 4])
 
-    def d_copy(h, z, m):
+    def seq_rows(s):
+        return pl.ds(pl.multiple_of(s * HALF, HALF), HALF)
+
+    def part_rows(part):
+        return pl.ds(0, ROWS) if part is None else seq_rows(y if part == 0 else 1 - y)
+
+    def d_copy(h, z, m, part=None):
         i = (h * 2 + z) * 3 + m
-        return remote(d_send.at[i], d_recv.at[i], d_s.at[i], d_r.at[i], core_peer)
-
-    def x_copy(h, m):
+        k = i if part != 1 else 12 + m
+        rows = part_rows(part)
+        return remote(d_send.at[i, rows], d_recv.at[i, rows], d_s.at[k], d_r.at[k], core_peer)
+
+    def x_copy(h, m, part=None):
         i = h * 3 + m
-        return remote(d_recv.at[h * 6 + m], x_recv.at[i], x_s.at[i], x_r.at[i], x_peer)
-
-    def o_copy(h, kind):
+        k = i if part != 1 else 6 + m
+        rows = part_rows(part)
+        return remote(d_recv.at[h * 6 + m, rows], x_recv.at[i, rows], x_s.at[k], x_r.at[k], x_peer)
+
+    def o_copy(h, kind, hh):
         slot = (t, t, rel[2])[kind]
-        i = h * 3 + kind
-        return remote(o_all.at[h, slot], o_all.at[h, slot], o_s.at[i], o_r.at[i], (core_peer, x_peer, core_peer)[kind])
-
-    def p_copy(h):
-        return remote(p_send.at[h], p_recv.at[h], p_s.at[h], p_r.at[h], y_peer)
+        i = (h * 3 + kind) * 2 + hh
+        ref = o_all.at[h, slot, :, pl.ds(hh * cols // 2, cols // 2)]
+        return remote(ref, ref, o_s.at[i], o_r.at[i], (core_peer, x_peer, core_peer)[kind])
+
+    def p_copy(h, nh):
+        cl = pl.ds(nh * 512, 512)
+        return remote(p_send.at[h, :, cl], p_recv.at[h, :, cl], p_s.at[h * 2 + nh], p_r.at[h * 2 + nh], y_peer)
 
     def s2_copy(h, k):
         i = h * 4 + k
@@ -169,44 +181,41 @@
     for k in range(1, 4):
         s1_copy(k).wait_recv()
     mean_o, rstd_o = moments((st1[0] + st1[1]) + (st1[2] + st1[3]))
-    for k in range(4, 8):
-        s1_copy(k).wait_recv()
-    mean_p, rstd_p = moments((st1[4] + st1[5]) + (st1[6] + st1[7]))
 
     def norm_rows(h, s, mean, rstd):
         sl = slice(h * HALF, (h + 1) * HALF)
         n = ((x_own(h, s) - mean[sl]) * rstd[sl]).astype(BF)
         n_buf[h, pl.ds(pl.multiple_of(s * HALF, HALF), HALF)] = n
 
-    def qkv_block(h, r, after):
+    def qkv_block(h, r, after, part=None, first=False):
         def body(m, carry):
-            if h == 0:
+            if first:
                 qkv_wait(r, m)
-            after(m, dot(n_buf[h], wbuf[r * 3 + m]))
+            after(m, dot(n_buf[h, part_rows(part)], wbuf[r * 3 + m]))
             return carry
 
         lax.fori_loop(0, 3, body, 0)
 
-    def qkv_send(h):
-        def give(z):
-            def after(m, res):
-                d_send[(h * 2 + z) * 3 + m] = res.astype(BF)
-                d_copy(h, z, m).start()
-            return after
-
-        def take(z):
-            def after(m, res):
-                d_copy(h, z, m).wait_recv()
-                i = (h * 2 + z) * 3 + m
-                d_recv[i] = (res + d_recv[i].astype(F32)).astype(BF)
-                if z == 0:
-                    x_copy(h, m).start()
-            return after
-
-        qkv_block(h, 3, give(0))
-        qkv_block(h, 2, take(0))
-        qkv_block(h, 1, give(1))
-        qkv_block(h, 0, take(1))
+    def give(h, z, part=None):
+        def after(m, res):
+            d_send[(h * 2 + z) * 3 + m, part_rows(part)] = res.astype(BF)
+            d_copy(h, z, m, part).start()
+        return after
+
+    def take(h, z, part=None):
+        def after(m, res):
+            d_copy(h, z, m, part).wait_recv()
+            i = (h * 2 + z) * 3 + m
+            rows = part_rows(part)
+            d_recv[i, rows] = (res + d_recv[i, rows].astype(F32)).astype(BF)
+            if z == 0:
+                if h == 0:
+                    x_copy(h, m, part).start()
+                else:
+                    @pl.when(m < 2)
+                    def _():
+                        x_copy(h, m).start()
+        return after
 
     def rotate(v, cos2, sin2):
         f = v.astype(F32)
@@ -214,7 +223,11 @@
 
     def attention(h):
         for m in range(3):
-            x_copy(h, m).wait_recv()
+            if h == 0:
+                x_copy(h, m, 0).wait_recv()
+                x_copy(h, m, 1).wait_recv()
+            else:
+                x_copy(h, m).wait_recv()
 
         def final(m):
             return (d_recv[h * 6 + 3 + m].astype(F32) + x_recv[h * 3 + m].astype(F32)).astype(BF)
@@ -243,26 +256,31 @@
                 e = jnp.exp(scores - jnp.max(scores, axis=1, keepdims=True))
                 prob = (e / jnp.sum(e, axis=1, keepdims=True)).astype(BF)
                 o_all[h, t, rs, cl] = dot(prob, vals).astype(BF)
-        o_copy(h, 1).start()
-        o_copy(h, 0).start()
+            if hd % 2 == 1:
+                o_copy(h, 1, hd // 2).start()
+                o_copy(h, 0, hd // 2).start()
 
     def relay_o(h):
-        o_copy(h, 1).wait_recv()
-        o_copy(h, 2).start()
+        for hh in range(2):
+            o_copy(h, 1, hh).wait_recv()
+            o_copy(h, 2, hh).start()
 
     def project_o(h):
-        o_copy(h, 0).wait_recv()
-        o_copy(h, 2).wait_recv()
+        for hh in range(2):
+            o_copy(h, 0, hh).wait_recv()
+        for hh in range(2):
+            o_copy(h, 2, hh).wait_recv()
         for nh in range(2):
             cl = slice(nh * 512, (nh + 1) * 512)
             res = jnp.zeros((ROWS, 512), F32)
             for b in range(4):
                 res = res + dot(o_all[h, b], wo_v[b * cols:(b + 1) * cols, cl])
             p_send[h, :, cl] = res.astype(BF)
-        p_copy(h).start()
+            p_copy(h, nh).start()
 
     def residual(h):
-        p_copy(h).wait_recv()
+        for nh in range(2):
+            p_copy(h, nh).wait_recv()
         attn = (p_send[h].astype(F32) + p_recv[h].astype(F32)).astype(BF).astype(F32)
         xv = jnp.concatenate([x_own(h, 0), x_own(h, 1)], axis=0)
         hv = (xv + attn).astype(BF)
@@ -283,9 +301,10 @@
 
     def gu_mul(h, j, w):
         slot = lax.rem(j, 2)
+        if h == 0:
+            for i in range(2):
+                gu_load(i, j, w).wait()
         for i, wv in enumerate((wg_v, wu_v)):
-            if h == 0:
-                gu_load(i, j, w).wait()
             for n0 in range(0, w, 512):
                 nw = min(512, w - n0)
                 start = j * FW + n0 if isinstance(j, int) else pl.multiple_of(j * FW + n0, 512)
@@ -302,18 +321,20 @@
             g_recv[i, k, :, 0:w] = (g_own[slot, k, :, 0:w] + g_recv[i, k, :, 0:w].astype(F32)).astype(BF)
         gx_copy(h, j, w).start()
 
-    def gate_up(h):
-        gu_mul(h, 0, FW)
+    def gate_up(h, j0, j1, last):
+        gu_mul(h, j0, FW)
 
         def body(j, carry):
             gu_mul(h, j, FW)
             gu_add(h, j - 1, FW)
             return carry
 
-        lax.fori_loop(1, n_full, body, 0)
-        gu_mul(h, n_full, last_w)
-        gu_add(h, n_full - 1, FW)
-        gu_add(h, n_full, last_w)
+        lax.fori_loop(j0 + 1, j1, body, 0)
+        if last:
+            gu_mul(h, n_full, last_w)
+        gu_add(h, j1 - 1, FW)
+        if last:
+            gu_add(h, n_full, last_w)
 
     def act(h, j, w):
         gx_copy(h, j, w).wait_recv()
@@ -333,32 +354,41 @@
     def down(h, j, w):
         a_copy(h, j, w, 0).wait_recv()
         a_copy(h, j, w, 2).wait_recv()
+        if h == 0:
+            for nh in range(2):
+                down_load(j, nh, w).wait()
         lhs = a_all[h * 6 + j, :, :, 0:w].reshape(ROWS, w)
         for nh in range(2):
-            if h == 0:
-                down_load(j, nh, w).wait()
             acc[h, :, nh * 512:(nh + 1) * 512] += dot(lhs, wbuf[j * 2 + nh, 0:w])
 
-    def mlp_out(h):
-        acc[h] = jnp.zeros((ROWS, width), F32)
-        act(h, 0, FW)
-        act(h, 1, FW)
-        relay_a(h, 0, FW)
-
+    def act_all(h):
         def body(j, carry):
             act(h, j, FW)
-            relay_a(h, j - 1, FW)
-            down(h, j - 2, FW)
             return carry
 
-        lax.fori_loop(2, n_full, body, 0)
+        lax.fori_loop(0, n_full, body, 0)
         act(h, n_full, last_w)
-        relay_a(h, n_full - 1, FW)
-        down(h, n_full - 2, FW)
+
+    def down_all(h, beside):
+        acc[h] = jnp.zeros((ROWS, width), F32)
+
+        def body(j, carry):
+            if beside is not None:
+                act(beside, j, FW)
+            relay_a(h, j, FW)
+
+            @pl.when(j > 0)
+            def _():
+                down(h, j - 1, FW)
+            return carry
+
+        lax.fori_loop(0, n_full, body, 0)
+        if beside is not None:
+            act(beside, n_full, last_w)
         relay_a(h, n_full, last_w)
         down(h, n_full - 1, FW)
         down(h, n_full, last_w)
-        f_send[h] = acc[h, pl.ds(pl.multiple_of((1 - y) * HALF, HALF), HALF)].astype(BF)
+        f_send[h] = acc[h, seq_rows(1 - y)].astype(BF)
         f_copy(h).start()
 
     def store_out(h):
@@ -369,22 +399,34 @@
         return pltpu.make_async_copy(y_buf.at[h], out_hbm.at[0, pl.ds(h * HALF, HALF)], ld_sem.at[h])
 
     norm_rows(0, y, mean_o, rstd_o)
+    qkv_block(0, 3, give(0, 0, 0), 0, True)
+    qkv_block(0, 2, take(0, 0, 0), 0, True)
+    for k in range(4, 8):
+        s1_copy(k).wait_recv()
+    mean_p, rstd_p = moments((st1[4] + st1[5]) + (st1[6] + st1[7]))
     xy_copy(0).wait_recv()
     norm_rows(0, 1 - y, mean_p, rstd_p)
-    qkv_send(0)
+    qkv_block(0, 3, give(0, 0, 1), 1)
+    qkv_block(0, 2, take(0, 0, 1), 1)
+    qkv_block(0, 1, give(0, 1), None, True)
+    qkv_block(0, 0, take(0, 1), None, True)
     for j in range(n_full + 1):
         for i in range(2):
             gu_load(i, j, FW if j < n_full else last_w).start()
     norm_rows(1, y, mean_o, rstd_o)
     xy_copy(1).wait_recv()
     norm_rows(1, 1 - y, mean_p, rstd_p)
-    qkv_send(1)
+    qkv_block(1, 3, give(1, 0))
+    qkv_block(1, 2, take(1, 0))
+    qkv_block(1, 1, give(1, 1))
+    qkv_block(1, 0, take(1, 1))
     for j in range(n_full + 1):
         for nh in range(2):
             down_load(j, nh, FW if j < n_full else last_w).start()
     for tb in tables:
         tb.wait()
     attention(0)
+    x_copy(1, 2).start()
     wo_load.wait()
     relay_o(0)
     project_o(0)
@@ -393,12 +435,14 @@
     relay_o(1)
     project_o(1)
     norm2(0)
-    gate_up(0)
+    gate_up(0, 0, 3, False)
     residual(1)
+    gate_up(0, 3, n_full, True)
     norm2(1)
-    gate_up(1)
-    mlp_out(0)
-    mlp_out(1)
+    gate_up(1, 0, n_full, True)
+    act_all(0)
+    down_all(0, 1)
+    down_all(1, None)
     stores = []
     for h in range(2):
         cp = store_out(h)
@@ -410,12 +454,15 @@
     for h in range(2):
         xy_copy(h).wait_send()
         for m in range(3):
-            d_copy(h, 0, m).wait_send()
+            for part in (0, 1) if h == 0 else (None,):
+                d_copy(h, 0, m, part).wait_send()
+                x_copy(h, m, part).wait_send()
             d_copy(h, 1, m).wait_send()
-            x_copy(h, m).wait_send()
-            o_copy(h, m).wait_send()
             s2_copy(h, m + 1).wait_send()
-        p_copy(h).wait_send()
+            for k in range(2):
+                o_copy(h, m, k).wait_send()
+        for nh in range(2):
+            p_copy(h, nh).wait_send()
         for j in range(n_full + 1):
             w = FW if j < n_full else last_w
             g_copy(h, j, w).wait_send()
@@ -474,8 +521,8 @@
                 vm((8, 8, 128), F32),
                 vm((2, 4, 8, 128), F32),
                 dma((4,)), dma((48,)),
-                dma((2,)), dma((2,)), dma((8,)), dma((8,)), dma((12,)), dma((12,)), dma((6,)), dma((6,)),
-                dma((6,)), dma((6,)), dma((2,)), dma((2,)), dma((8,)), dma((8,)), dma((12,)), dma((12,)),
+                dma((2,)), dma((2,)), dma((8,)), dma((8,)), dma((15,)), dma((15,)), dma((9,)), dma((9,)),
+                dma((12,)), dma((12,)), dma((4,)), dma((4,)), dma((8,)), dma((8,)), dma((12,)), dma((12,)),
                 dma((12,)), dma((12,)), dma((36,)), dma((36,)), dma((2,)), dma((2,)),
             ],
             compiler_params=pltpu.CompilerParams(collective_id=0, has_side_effects=True, vmem_limit_bytes=67043328),

time: 123 us -> 103 us (0.84)
  Pallas kernels: 121 us -> 102 us
    pallas_call x1, Pallas kernels: 121 us -> 102 us  [layer_fn(): pl.pallas_call(layer_kernel, out_shape=jax.ShapeDtypeStruct(x_blk.shape,...]
where the time goes in v2:
time: 103 us
  Pallas kernels  102 us (99%)
  local copies, waits for them, and re-layouts  1.67 us (2%)
    pallas_call x1, Pallas kernels, layer_fn(): pl.pallas_call(layer_kernel, out_shape=jax.ShapeDtypeStruct(x_blk.shape,...  102 us

profile of v2, /device:TPU:0, one launch (start us, length us, event | category | flops | bytes accessed | tf_op | source)
XLA Modules:
  0.0 103.3 jit_solution(5458776890471826180)
XLA Ops:
  0.0 101.6 %layer.1 = bf16[1,128,1024]{2,1,0:T(8,128)(2,1)} custom-call(bf16[1,128,1024]{2,1,0:T(8,128)(2,1)} %x_hbm.1, bf16[1024,2048]{1,0:T(8,128)(2,1)} %wq_hbm.1, bf16[1024,2048]{1,0:T(8,128)(2,1)} %wk_hbm.1, bf16[1024,2048]{1,0:T(8,128)(2,1)} %wv_hbm.1, bf16[2048,1024]{1,0:T(8,128)(2,1)} %wo_hbm.1, bf16[1024,5504]{1,0:T(8,128)(2,1)} %wg_hbm.1, ...), custom_call_target="tpu_custom_call" | custom-call | tf_op jit(solution)/shard_map/layer/pallas_call | solution.py:489
  101.6 1.7 %copy.12 = bf16[1,128,1024]{2,1,0:T(8,128)(2,1)} copy(bf16[1,128,1024]{2,1,0:T(8,128)(2,1)} %layer.1) | data formatting | bytes 524288

commit v3 on v2

--- a/solution.py
+++ b/solution.py
@@ -14,9 +14,10 @@
 F32 = jnp.float32
 MESH = pl.DeviceIdType.MESH
 
-HALF = 64
-ROWS = 128
-SUB = 32
+NCH = 4
+TOK = 32
+ROWS = 2 * TOK
+SUB = ROWS // 4
 FW = 1024
 
 
@@ -62,9 +63,9 @@
         return pltpu.make_async_remote_copy(src_ref=src, dst_ref=dst, send_sem=ss, recv_sem=rs, device_id=dev, device_id_type=MESH)
 
     def x_load(h):
-        return pltpu.make_async_copy(x_hbm.at[0, pl.ds(h * HALF, HALF)], x_all.at[h, y], ld_sem.at[h])
-
-    tables = [pltpu.make_async_copy(cos_hbm, cos_v, ld_sem.at[2]), pltpu.make_async_copy(sin_hbm, sin_v, ld_sem.at[3])]
+        return pltpu.make_async_copy(x_hbm.at[0, pl.ds(h * TOK, TOK)], x_all.at[h, y], ld_sem.at[h])
+
+    tables = [pltpu.make_async_copy(cos_hbm, cos_v, ld_sem.at[NCH]), pltpu.make_async_copy(sin_hbm, sin_v, ld_sem.at[NCH + 1])]
 
     def qkv_load(r, m):
         src = (wq_hbm, wk_hbm, wv_hbm)[m].at[:, pl.ds(pl.multiple_of(rel[r] * cols, cols), cols)]
@@ -91,22 +92,15 @@
         return remote(st1.at[0], st1.at[k], s1_s.at[k], s1_r.at[k], peer[k] if k < 4 else other[k - 4])
 
     def seq_rows(s):
-        return pl.ds(pl.multiple_of(s * HALF, HALF), HALF)
-
-    def part_rows(part):
-        return pl.ds(0, ROWS) if part is None else seq_rows(y if part == 0 else 1 - y)
-
-    def d_copy(h, z, m, part=None):
+        return pl.ds(pl.multiple_of(s * TOK, TOK), TOK)
+
+    def d_copy(h, z, m):
         i = (h * 2 + z) * 3 + m
-        k = i if part != 1 else 12 + m
-        rows = part_rows(part)
-        return remote(d_send.at[i, rows], d_recv.at[i, rows], d_s.at[k], d_r.at[k], core_peer)
-
-    def x_copy(h, m, part=None):
+        return remote(d_send.at[i], d_recv.at[i], d_s.at[i], d_r.at[i], core_peer)
+
+    def x_copy(h, m):
         i = h * 3 + m
-        k = i if part != 1 else 6 + m
-        rows = part_rows(part)
-        return remote(d_recv.at[h * 6 + m, rows], x_recv.at[i, rows], x_s.at[k], x_r.at[k], x_peer)
+        return remote(d_recv.at[h * 6 + m], x_recv.at[i], x_s.at[i], x_r.at[i], x_peer)
 
     def o_copy(h, kind, hh):
         slot = (t, t, rel[2])[kind]
@@ -146,7 +140,10 @@
     def local_stats(v):
         s = jnp.sum(v, axis=1, keepdims=True)
         q = jnp.sum(v * v, axis=1, keepdims=True)
-        m = jnp.where(lane == 0, s, jnp.where(lane == 1, q, 0.0))
+        n = v.shape[0]
+        m = jnp.where(lane[0:n] == 0, s, jnp.where(lane[0:n] == 1, q, 0.0))
+        if n < 128:
+            m = jnp.concatenate([m, jnp.zeros((128 - n, 128), F32)], axis=0)
         return m.T[0:8]
 
     def moments(total):
@@ -159,7 +156,7 @@
     def x_own(h, s):
         return x_all[h, s].astype(F32)
 
-    for h in range(2):
+    for h in range(NCH):
         x_load(h).start()
     for r in (3, 2, 1, 0):
         for m in range(3):
@@ -169,13 +166,13 @@
     barrier = pltpu.get_barrier_semaphore()
     for dev in peer[1:] + other:
         pl.semaphore_signal(barrier, inc=1, device_id=dev, device_id_type=MESH)
-    for h in range(2):
+    for h in range(NCH):
         x_load(h).wait()
-    st1[0] = local_stats(jnp.concatenate([x_own(0, y), x_own(1, y)], axis=0))
+    st1[0] = local_stats(jnp.concatenate([x_own(h, y) for h in range(NCH)], axis=0))
     pl.semaphore_wait(barrier, 7)
     for k in range(1, 8):
         s1_copy(k).start()
-    for h in range(2):
+    for h in range(NCH):
         xy_copy(h).start()
     wo_load.start()
     for k in range(1, 4):
@@ -183,39 +180,47 @@
     mean_o, rstd_o = moments((st1[0] + st1[1]) + (st1[2] + st1[3]))
 
     def norm_rows(h, s, mean, rstd):
-        sl = slice(h * HALF, (h + 1) * HALF)
+        sl = slice(h * TOK, (h + 1) * TOK)
         n = ((x_own(h, s) - mean[sl]) * rstd[sl]).astype(BF)
-        n_buf[h, pl.ds(pl.multiple_of(s * HALF, HALF), HALF)] = n
-
-    def qkv_block(h, r, after, part=None, first=False):
+        n_buf[h, pl.ds(pl.multiple_of(s * TOK, TOK), TOK)] = n
+
+    def qkv_block(h, r, after):
         def body(m, carry):
-            if first:
+            if h == 0:
                 qkv_wait(r, m)
-            after(m, dot(n_buf[h, part_rows(part)], wbuf[r * 3 + m]))
+            after(m, dot(n_buf[h], wbuf[r * 3 + m]))
             return carry
 
         lax.fori_loop(0, 3, body, 0)
 
-    def give(h, z, part=None):
+    def give(h, z):
         def after(m, res):
-            d_send[(h * 2 + z) * 3 + m, part_rows(part)] = res.astype(BF)
-            d_copy(h, z, m, part).start()
+            d_send[(h * 2 + z) * 3 + m] = res.astype(BF)
+            d_copy(h, z, m).start()
         return after
 
-    def take(h, z, part=None):
+    def take(h, z):
         def after(m, res):
-            d_copy(h, z, m, part).wait_recv()
+            d_copy(h, z, m).wait_recv()
             i = (h * 2 + z) * 3 + m
-            rows = part_rows(part)
-            d_recv[i, rows] = (res + d_recv[i, rows].astype(F32)).astype(BF)
+            d_recv[i] = (res + d_recv[i].astype(F32)).astype(BF)
             if z == 0:
-                if h == 0:
-                    x_copy(h, m, part).start()
-                else:
-                    @pl.when(m < 2)
-                    def _():
-                        x_copy(h, m).start()
+                x_copy(h, m).start()
         return after
+
+    def qkv_far(h):
+        if h == 0:
+            norm_rows(0, y, mean_o, rstd_o)
+        xy_copy(h).wait_recv()
+        norm_rows(h, 1 - y, mean_p, rstd_p)
+        if h > 0:
+            norm_rows(h, y, mean_o, rstd_o)
+        qkv_block(h, 3, give(h, 0))
+        qkv_block(h, 2, take(h, 0))
+
+    def qkv_near(h):
+        qkv_block(h, 1, give(h, 1))
+        qkv_block(h, 0, take(h, 1))
 
     def rotate(v, cos2, sin2):
         f = v.astype(F32)
@@ -223,34 +228,30 @@
 
     def attention(h):
         for m in range(3):
-            if h == 0:
-                x_copy(h, m, 0).wait_recv()
-                x_copy(h, m, 1).wait_recv()
-            else:
-                x_copy(h, m).wait_recv()
+            x_copy(h, m).wait_recv()
 
         def final(m):
             return (d_recv[h * 6 + 3 + m].astype(F32) + x_recv[h * 3 + m].astype(F32)).astype(BF)
 
-        sl = slice(h * HALF, (h + 1) * HALF)
-        n_keys = (h + 1) * HALF
+        sl = slice(h * TOK, (h + 1) * TOK)
+        n_keys = (h + 1) * TOK
         cos2 = jnp.concatenate([cos_v[sl], cos_v[sl]], axis=0)
         sin2 = jnp.concatenate([sin_v[sl], sin_v[sl]], axis=0)
         q, k, v = final(0), final(1), final(2)
         for s in range(2):
-            v_buf[s, sl] = v[s * HALF:(s + 1) * HALF]
-        q_pos = h * HALF + lax.broadcasted_iota(jnp.int32, (HALF, n_keys), 0)
-        k_pos = lax.broadcasted_iota(jnp.int32, (HALF, n_keys), 1)
+            v_buf[s, sl] = v[s * TOK:(s + 1) * TOK]
+        q_pos = h * TOK + lax.broadcasted_iota(jnp.int32, (TOK, n_keys), 0)
+        k_pos = lax.broadcasted_iota(jnp.int32, (TOK, n_keys), 1)
         allowed = q_pos >= k_pos
         for hd in range(cols // HEAD_DIM):
             cl = slice(hd * HEAD_DIM, (hd + 1) * HEAD_DIM)
             qr = rotate(q[:, cl], cos2, sin2)
             kr = rotate(k[:, cl], cos2, sin2)
             for s in range(2):
-                rs = slice(s * HALF, (s + 1) * HALF)
+                rs = slice(s * TOK, (s + 1) * TOK)
                 k_buf[s, sl, cl] = kr[rs]
-                keys = kr[rs] if h == 0 else jnp.concatenate([k_buf[s, 0:HALF, cl], kr[rs]], axis=0)
-                vals = v[rs, cl] if h == 0 else jnp.concatenate([v_buf[s, 0:HALF, cl], v[rs, cl]], axis=0)
+                keys = k_buf[s, 0:n_keys, cl]
+                vals = v_buf[s, 0:n_keys, cl]
                 scores = dot_t(qr[rs], keys) * (HEAD_DIM ** -0.5)
                 scores = jnp.where(allowed, scores, -1e30)
                 e = jnp.exp(scores - jnp.max(scores, axis=1, keepdims=True))
@@ -260,10 +261,9 @@
                 o_copy(h, 1, hd // 2).start()
                 o_copy(h, 0, hd // 2).start()
 
-    def relay_o(h):
-        for hh in range(2):
-            o_copy(h, 1, hh).wait_recv()
-            o_copy(h, 2, hh).start()
+    def relay_o(h, hh):
+        o_copy(h, 1, hh).wait_recv()
+        o_copy(h, 2, hh).start()
 
     def project_o(h):
         for hh in range(2):
@@ -293,14 +293,14 @@
         for k in range(1, 4):
             s2_copy(h, k).wait_recv()
         mean, rstd = moments((st2[h, 0] + st2[h, 1]) + (st2[h, 2] + st2[h, 3]))
-        n = ((h_buf[h].astype(F32) - mean) * rstd).astype(BF)
+        n = ((h_buf[h].astype(F32) - mean[0:ROWS]) * rstd[0:ROWS]).astype(BF)
         for b in range(4):
             e_c = c if b // 2 == 1 else 1 - c
             e_x = xc if b % 2 == 1 else 1 - xc
-            n_buf[h, pl.ds(pl.multiple_of(64 * e_c + 32 * e_x, SUB), SUB)] = n[b * SUB:(b + 1) * SUB]
+            n_buf[h, pl.ds(pl.multiple_of(2 * SUB * e_c + SUB * e_x, SUB), SUB)] = n[b * SUB:(b + 1) * SUB]
 
     def gu_mul(h, j, w):
-        slot = lax.rem(j, 2)
+        slot = (h * 6 + j) % 4 if isinstance(j, int) else lax.rem(h * 6 + j, 4)
         if h == 0:
             for i in range(2):
                 gu_load(i, j, w).wait()
@@ -309,32 +309,36 @@
                 nw = min(512, w - n0)
                 start = j * FW + n0 if isinstance(j, int) else pl.multiple_of(j * FW + n0, 512)
                 res = dot(n_buf[h], wv[:, pl.ds(start, nw)])
-                g_send[h * 6 + j, i, :, n0:n0 + nw] = res[0:64].astype(BF)
-                g_own[slot, i, :, n0:n0 + nw] = res[64:128]
+                g_send[h * 6 + j, i, :, n0:n0 + nw] = res[0:2 * SUB].astype(BF)
+                g_own[slot, i, :, n0:n0 + nw] = res[2 * SUB:ROWS]
         g_copy(h, j, w).start()
 
     def gu_add(h, j, w):
-        slot = lax.rem(j, 2)
+        slot = (h * 6 + j) % 4 if isinstance(j, int) else lax.rem(h * 6 + j, 4)
         g_copy(h, j, w).wait_recv()
         i = h * 6 + j
         for k in range(2):
             g_recv[i, k, :, 0:w] = (g_own[slot, k, :, 0:w] + g_recv[i, k, :, 0:w].astype(F32)).astype(BF)
         gx_copy(h, j, w).start()
 
-    def gate_up(h, j0, j1, last):
-        gu_mul(h, j0, FW)
-
+    def gu_loop(h, j0, j1):
         def body(j, carry):
             gu_mul(h, j, FW)
-            gu_add(h, j - 1, FW)
+
+            @pl.when(j >= 2)
+            def _():
+                gu_add(h, j - 2, FW)
             return carry
 
-        lax.fori_loop(j0 + 1, j1, body, 0)
-        if last:
-            gu_mul(h, n_full, last_w)
-        gu_add(h, j1 - 1, FW)
-        if last:
-            gu_add(h, n_full, last_w)
+        lax.fori_loop(j0, j1, body, 0)
+
+    def gu_last(h):
+        gu_mul(h, n_full, last_w)
+        gu_add(h, n_full - 2, FW)
+
+    def gu_flush(h):
+        gu_add(h, n_full - 1, FW)
+        gu_add(h, n_full, last_w)
 
     def act(h, j, w):
         gx_copy(h, j, w).wait_recv()
@@ -392,72 +396,92 @@
         f_copy(h).start()
 
     def store_out(h):
-        own = pl.ds(pl.multiple_of(y * HALF, HALF), HALF)
+        own = pl.ds(pl.multiple_of(y * TOK, TOK), TOK)
         f_copy(h).wait_recv()
         mlp = (acc[h, own].astype(BF).astype(F32) + f_recv[h].astype(F32)).astype(BF).astype(F32)
         y_buf[h] = (h_buf[h, own].astype(F32) + mlp).astype(BF)
-        return pltpu.make_async_copy(y_buf.at[h], out_hbm.at[0, pl.ds(h * HALF, HALF)], ld_sem.at[h])
-
-    norm_rows(0, y, mean_o, rstd_o)
-    qkv_block(0, 3, give(0, 0, 0), 0, True)
-    qkv_block(0, 2, take(0, 0, 0), 0, True)
+        return pltpu.make_async_copy(y_buf.at[h], out_hbm.at[0, pl.ds(h * TOK, TOK)], ld_sem.at[h])
+
     for k in range(4, 8):
         s1_copy(k).wait_recv()
     mean_p, rstd_p = moments((st1[4] + st1[5]) + (st1[6] + st1[7]))
-    xy_copy(0).wait_recv()
-    norm_rows(0, 1 - y, mean_p, rstd_p)
-    qkv_block(0, 3, give(0, 0, 1), 1)
-    qkv_block(0, 2, take(0, 0, 1), 1)
-    qkv_block(0, 1, give(0, 1), None, True)
-    qkv_block(0, 0, take(0, 1), None, True)
+    qkv_far(0)
+    qkv_near(0)
     for j in range(n_full + 1):
         for i in range(2):
             gu_load(i, j, FW if j < n_full else last_w).start()
-    norm_rows(1, y, mean_o, rstd_o)
-    xy_copy(1).wait_recv()
-    norm_rows(1, 1 - y, mean_p, rstd_p)
-    qkv_block(1, 3, give(1, 0))
-    qkv_block(1, 2, take(1, 0))
-    qkv_block(1, 1, give(1, 1))
-    qkv_block(1, 0, take(1, 1))
+    qkv_far(1)
+    qkv_near(1)
+    for tb in tables:
+        tb.wait()
+    attention(0)
+    qkv_far(2)
+    attention(1)
+    relay_o(0, 0)
+    qkv_near(2)
+    relay_o(0, 1)
+    qkv_far(3)
+    wo_load.wait()
+    project_o(0)
+    relay_o(1, 0)
+    attention(2)
+    relay_o(1, 1)
+    qkv_near(3)
     for j in range(n_full + 1):
         for nh in range(2):
             down_load(j, nh, FW if j < n_full else last_w).start()
-    for tb in tables:
-        tb.wait()
-    attention(0)
-    x_copy(1, 2).start()
-    wo_load.wait()
-    relay_o(0)
-    project_o(0)
-    attention(1)
+    project_o(1)
     residual(0)
-    relay_o(1)
-    project_o(1)
+    attention(3)
+    relay_o(2, 0)
+    relay_o(2, 1)
     norm2(0)
-    gate_up(0, 0, 3, False)
+    project_o(2)
+    gu_loop(0, 0, 1)
+    relay_o(3, 0)
+    relay_o(3, 1)
     residual(1)
-    gate_up(0, 3, n_full, True)
+    project_o(3)
+    gu_loop(0, 1, 5)
     norm2(1)
-    gate_up(1, 0, n_full, True)
+    residual(2)
+    gu_last(0)
+    gu_loop(1, 0, 1)
+    gu_flush(0)
+    residual(3)
+    gu_loop(1, 1, 5)
+    norm2(2)
+    gu_last(1)
+    gu_loop(2, 0, 1)
+    gu_flush(1)
+    gu_loop(2, 1, 5)
+    norm2(3)
+    gu_last(2)
+    gu_loop(3, 0, 1)
+    gu_flush(2)
+    gu_loop(3, 1, 5)
+    gu_last(3)
+    gu_flush(3)
     act_all(0)
-    down_all(0, 1)
-    down_all(1, None)
+    act_all(1)
+    down_all(0, 2)
+    down_all(1, 3)
+    down_all(2, None)
+    down_all(3, None)
     stores = []
-    for h in range(2):
+    for h in range(NCH):
         cp = store_out(h)
         cp.start()
         stores.append(cp)
 
     for k in range(1, 8):
         s1_copy(k).wait_send()
-    for h in range(2):
+    for h in range(NCH):
         xy_copy(h).wait_send()
         for m in range(3):
-            for part in (0, 1) if h == 0 else (None,):
-                d_copy(h, 0, m, part).wait_send()
-                x_copy(h, m, part).wait_send()
+            d_copy(h, 0, m).wait_send()
             d_copy(h, 1, m).wait_send()
+            x_copy(h, m).wait_send()
             s2_copy(h, m + 1).wait_send()
             for k in range(2):
                 o_copy(h, m, k).wait_send()
@@ -498,32 +522,30 @@
                 vm(w_up.shape, BF),
                 vm((seq_len, HEAD_DIM), F32),
                 vm((seq_len, HEAD_DIM), F32),
-                vm((2, 2, HALF, width), BF),
-                vm((2, ROWS, width), BF),
-                vm((12, ROWS, cols), BF),
-                vm((12, ROWS, cols), BF),
-                vm((6, ROWS, cols), BF),
+                vm((NCH, 2, TOK, width), BF),
+                vm((NCH, ROWS, width), BF),
+                vm((6 * NCH, ROWS, cols), BF),
+                vm((6 * NCH, ROWS, cols), BF),
+                vm((3 * NCH, ROWS, cols), BF),
                 vm((2, seq_len, cols), BF),
                 vm((2, seq_len, cols), BF),
-                vm((2, 4, ROWS, cols), BF),
-                vm((2, ROWS, width), BF),
-                vm((2, ROWS, width), BF),
-                vm((2, ROWS, width), BF),
-                vm((12, 2, 2 * SUB, FW), BF),
-                vm((12, 2, 2 * SUB, FW), BF),
-                vm((2, 2, 2 * SUB, FW), F32),
-                vm((12, 2, SUB, FW), BF),
-                vm((12, 4, SUB, FW), BF),
-                vm((2, ROWS, width), F32),
-                vm((2, HALF, width), BF),
-                vm((2, HALF, width), BF),
-                vm((2, HALF, width), BF),
+                vm((NCH, 4, ROWS, cols), BF),
+                vm((NCH, ROWS, width), BF),
+                vm((NCH, ROWS, width), BF),
+                vm((NCH, ROWS, width), BF),
+                vm((6 * NCH, 2, 2 * SUB, FW), BF),
+                vm((6 * NCH, 2, 2 * SUB, FW), BF),
+                vm((4, 2, 2 * SUB, FW), F32),
+                vm((6 * NCH, 2, SUB, FW), BF),
+                vm((6 * NCH, 4, SUB, FW), BF),
+                vm((NCH, ROWS, width), F32),
+                vm((NCH, TOK, width), BF),
+                vm((NCH, TOK, width), BF),
+                vm((NCH, TOK, width), BF),
                 vm((8, 8, 128), F32),
-                vm((2, 4, 8, 128), F32),
-                dma((4,)), dma((48,)),
-                dma((2,)), dma((2,)), dma((8,)), dma((8,)), dma((15,)), dma((15,)), dma((9,)), dma((9,)),
-                dma((12,)), dma((12,)), dma((4,)), dma((4,)), dma((8,)), dma((8,)), dma((12,)), dma((12,)),
-                dma((12,)), dma((12,)), dma((36,)), dma((36,)), dma((2,)), dma((2,)),
+                vm((NCH, 4, 8, 128), F32),
+                dma((NCH + 2,)), dma((48,)),
+                *(dma((n,)) for n in (NCH, 8, 6 * NCH, 3 * NCH, 6 * NCH, 2 * NCH, 4 * NCH, 6 * NCH, 6 * NCH, 18 * NCH, NCH) for _ in range(2)),
             ],
             compiler_params=pltpu.CompilerParams(collective_id=0, has_side_effects=True, vmem_limit_bytes=67043328),
             name="layer",

time: 103 us -> 112 us (1.087)
  Pallas kernels: 102 us -> 111 us
    pallas_call x1, Pallas kernels: 102 us -> 111 us  [layer_fn(): pl.pallas_call(layer_kernel, out_shape=jax.ShapeDtypeStruct(x_blk.shape,...]
where the time goes in v3:
time: 112 us
  Pallas kernels  111 us (99%)
  local copies, waits for them, and re-layouts  1.67 us (1%)
    pallas_call x1, Pallas kernels, layer_fn(): pl.pallas_call(layer_kernel, out_shape=jax.ShapeDtypeStruct(x_blk.shape,...  111 us

profile of v3, /device:TPU:0, one launch (start us, length us, event | category | flops | bytes accessed | tf_op | source)
XLA Modules:
  0.0 112.3 jit_solution(6320060580488875608)
XLA Ops:
  0.0 110.6 %layer.1 = bf16[1,128,1024]{2,1,0:T(8,128)(2,1)} custom-call(bf16[1,128,1024]{2,1,0:T(8,128)(2,1)} %x_hbm.1, bf16[1024,2048]{1,0:T(8,128)(2,1)} %wq_hbm.1, bf16[1024,2048]{1,0:T(8,128)(2,1)} %wk_hbm.1, bf16[1024,2048]{1,0:T(8,128)(2,1)} %wv_hbm.1, bf16[2048,1024]{1,0:T(8,128)(2,1)} %wo_hbm.1, bf16[1024,5504]{1,0:T(8,128)(2,1)} %wg_hbm.1, ...), custom_call_target="tpu_custom_call" | custom-call | tf_op jit(solution)/shard_map/layer/pallas_call | solution.py:513
  110.6 1.7 %copy.12 = bf16[1,128,1024]{2,1,0:T(8,128)(2,1)} copy(bf16[1,128,1024]{2,1,0:T(8,128)(2,1)} %layer.1) | data formatting | bytes 524288

commit v4 on v3

--- a/solution.py
+++ b/solution.py
@@ -102,10 +102,10 @@
         i = h * 3 + m
         return remote(d_recv.at[h * 6 + m], x_recv.at[i], x_s.at[i], x_r.at[i], x_peer)
 
-    def o_copy(h, kind, hh):
+    def o_copy(h, kind):
         slot = (t, t, rel[2])[kind]
-        i = (h * 3 + kind) * 2 + hh
-        ref = o_all.at[h, slot, :, pl.ds(hh * cols // 2, cols // 2)]
+        i = h * 3 + kind
+        ref = o_all.at[h, slot]
         return remote(ref, ref, o_s.at[i], o_r.at[i], (core_peer, x_peer, core_peer)[kind])
 
     def p_copy(h, nh):
@@ -208,19 +208,37 @@
                 x_copy(h, m).start()
         return after
 
-    def qkv_far(h):
-        if h == 0:
-            norm_rows(0, y, mean_o, rstd_o)
+    def norm_chunk(h):
+        norm_rows(h, y, mean_o, rstd_o)
         xy_copy(h).wait_recv()
         norm_rows(h, 1 - y, mean_p, rstd_p)
-        if h > 0:
-            norm_rows(h, y, mean_o, rstd_o)
-        qkv_block(h, 3, give(h, 0))
-        qkv_block(h, 2, take(h, 0))
-
-    def qkv_near(h):
-        qkv_block(h, 1, give(h, 1))
-        qkv_block(h, 0, take(h, 1))
+
+    def qkv_first():
+        norm_chunk(0)
+        qkv_block(0, 3, give(0, 0))
+        qkv_block(0, 2, take(0, 0))
+        qkv_block(0, 1, give(0, 1))
+        qkv_block(0, 0, take(0, 1))
+
+    def qkv_give(h):
+        norm_chunk(h)
+        for z in range(2):
+            for m in range(3):
+                d_send[(h * 2 + z) * 3 + m] = dot(n_buf[h], wbuf[(3 - 2 * z) * 3 + m]).astype(BF)
+            for m in range(3):
+                d_copy(h, z, m).start()
+
+    def qkv_take(h, z):
+        own = [dot(n_buf[h], wbuf[(2 - 2 * z) * 3 + m]) for m in range(3)]
+        for m in range(3):
+            d_copy(h, z, m).wait_recv()
+        for m in range(3):
+            i = (h * 2 + z) * 3 + m
+            d_recv[i] = (own[m] + d_recv[i].astype(F32)).astype(BF)
+
+    def qkv_send(h):
+        for m in range(3):
+            x_copy(h, m).start()
 
     def rotate(v, cos2, sin2):
         f = v.astype(F32)
@@ -240,36 +258,33 @@
         q, k, v = final(0), final(1), final(2)
         for s in range(2):
             v_buf[s, sl] = v[s * TOK:(s + 1) * TOK]
-        q_pos = h * TOK + lax.broadcasted_iota(jnp.int32, (TOK, n_keys), 0)
-        k_pos = lax.broadcasted_iota(jnp.int32, (TOK, n_keys), 1)
-        allowed = q_pos >= k_pos
-        for hd in range(cols // HEAD_DIM):
-            cl = slice(hd * HEAD_DIM, (hd + 1) * HEAD_DIM)
-            qr = rotate(q[:, cl], cos2, sin2)
-            kr = rotate(k[:, cl], cos2, sin2)
-            for s in range(2):
-                rs = slice(s * TOK, (s + 1) * TOK)
-                k_buf[s, sl, cl] = kr[rs]
-                keys = k_buf[s, 0:n_keys, cl]
-                vals = v_buf[s, 0:n_keys, cl]
-                scores = dot_t(qr[rs], keys) * (HEAD_DIM ** -0.5)
-                scores = jnp.where(allowed, scores, -1e30)
-                e = jnp.exp(scores - jnp.max(scores, axis=1, keepdims=True))
-                prob = (e / jnp.sum(e, axis=1, keepdims=True)).astype(BF)
-                o_all[h, t, rs, cl] = dot(prob, vals).astype(BF)
-            if hd % 2 == 1:
-                o_copy(h, 1, hd // 2).start()
-                o_copy(h, 0, hd // 2).start()
-
-    def relay_o(h, hh):
-        o_copy(h, 1, hh).wait_recv()
-        o_copy(h, 2, hh).start()
+        heads = [slice(hd * HEAD_DIM, (hd + 1) * HEAD_DIM) for hd in range(cols // HEAD_DIM)]
+        blocks = [(hd, s) for hd in range(len(heads)) for s in range(2)]
+        qr = [rotate(q[:, cl], cos2, sin2) for cl in heads]
+        kr = [rotate(k[:, cl], cos2, sin2) for cl in heads]
+        for hd, s in blocks:
+            k_buf[s, sl, heads[hd]] = kr[hd][s * TOK:(s + 1) * TOK]
+        scores = jnp.concatenate(
+            [dot_t(qr[hd][s * TOK:(s + 1) * TOK], k_buf[s, 0:n_keys, heads[hd]]) for hd, s in blocks], axis=0
+        ) * (HEAD_DIM ** -0.5)
+        q_pos = h * TOK + lax.rem(lax.broadcasted_iota(jnp.int32, scores.shape, 0), TOK)
+        k_pos = lax.broadcasted_iota(jnp.int32, scores.shape, 1)
+        scores = jnp.where(q_pos >= k_pos, scores, -1e30)
+        e = jnp.exp(scores - jnp.max(scores, axis=1, keepdims=True))
+        prob = (e / jnp.sum(e, axis=1, keepdims=True)).astype(BF)
+        for i, (hd, s) in enumerate(blocks):
+            o = dot(prob[i * TOK:(i + 1) * TOK], v_buf[s, 0:n_keys, heads[hd]])
+            o_all[h, t, s * TOK:(s + 1) * TOK, heads[hd]] = o.astype(BF)
+        o_copy(h, 1).start()
+        o_copy(h, 0).start()
+
+    def relay_o(h):
+        o_copy(h, 1).wait_recv()
+        o_copy(h, 2).start()
 
     def project_o(h):
-        for hh in range(2):
-            o_copy(h, 0, hh).wait_recv()
-        for hh in range(2):
-            o_copy(h, 2, hh).wait_recv()
+        o_copy(h, 0).wait_recv()
+        o_copy(h, 2).wait_recv()
         for nh in range(2):
             cl = slice(nh * 512, (nh + 1) * 512)
             res = jnp.zeros((ROWS, 512), F32)
@@ -321,16 +336,19 @@
             g_recv[i, k, :, 0:w] = (g_own[slot, k, :, 0:w] + g_recv[i, k, :, 0:w].astype(F32)).astype(BF)
         gx_copy(h, j, w).start()
 
-    def gu_loop(h, j0, j1):
+    def gu_loop(h, j0, j1, lag=2, first=0):
         def body(j, carry):
             gu_mul(h, j, FW)
 
-            @pl.when(j >= 2)
+            @pl.when(j >= lag + first)
             def _():
-                gu_add(h, j - 2, FW)
+                gu_add(h, j - lag, FW)
             return carry
 
-        lax.fori_loop(j0, j1, body, 0)
+        if j1 - j0 == 1 and j0 < lag + first:
+            gu_mul(h, j0, FW)
+        else:
+            lax.fori_loop(j0, j1, body, 0)
 
     def gu_last(h):
         gu_mul(h, n_full, last_w)
@@ -373,27 +391,47 @@
         lax.fori_loop(0, n_full, body, 0)
         act(h, n_full, last_w)
 
+    def relay_all(h):
+        def body(j, carry):
+            relay_a(h, j, FW)
+            return carry
+
+        lax.fori_loop(0, n_full, body, 0)
+        relay_a(h, n_full, last_w)
+
     def down_all(h, beside):
         acc[h] = jnp.zeros((ROWS, width), F32)
 
         def body(j, carry):
-            if beside is not None:
-                act(beside, j, FW)
+            act(beside, j, FW)
+            down(h, j, FW)
+            return carry
+
+        lax.fori_loop(0, n_full, body, 0)
+        act(beside, n_full, last_w)
+        down(h, n_full, last_w)
+        down_send(h)
+
+    def down_send(h):
+        f_send[h] = acc[h, seq_rows(1 - y)].astype(BF)
+        f_copy(h).start()
+
+    def relay_down(h):
+        acc[h] = jnp.zeros((ROWS, width), F32)
+        relay_a(h, 0, FW)
+        relay_a(h, 1, FW)
+
+        def body(j, carry):
             relay_a(h, j, FW)
-
-            @pl.when(j > 0)
-            def _():
-                down(h, j - 1, FW)
+            down(h, j - 2, FW)
             return carry
 
-        lax.fori_loop(0, n_full, body, 0)
-        if beside is not None:
-            act(beside, n_full, last_w)
+        lax.fori_loop(2, n_full, body, 0)
         relay_a(h, n_full, last_w)
+        down(h, n_full - 2, FW)
         down(h, n_full - 1, FW)
         down(h, n_full, last_w)
-        f_send[h] = acc[h, seq_rows(1 - y)].astype(BF)
-        f_copy(h).start()
+        down_send(h)
 
     def store_out(h):
         own = pl.ds(pl.multiple_of(y * TOK, TOK), TOK)
@@ -405,69 +443,75 @@
     for k in range(4, 8):
         s1_copy(k).wait_recv()
     mean_p, rstd_p = moments((st1[4] + st1[5]) + (st1[6] + st1[7]))
-    qkv_far(0)
-    qkv_near(0)
+    qkv_first()
     for j in range(n_full + 1):
         for i in range(2):
             gu_load(i, j, FW if j < n_full else last_w).start()
-    qkv_far(1)
-    qkv_near(1)
+    qkv_give(1)
+    qkv_take(1, 0)
+    qkv_send(1)
+    qkv_take(1, 1)
     for tb in tables:
         tb.wait()
+    qkv_give(2)
+    qkv_take(2, 0)
     attention(0)
-    qkv_far(2)
+    qkv_send(2)
+    qkv_take(2, 1)
+    qkv_give(3)
+    qkv_take(3, 0)
     attention(1)
-    relay_o(0, 0)
-    qkv_near(2)
-    relay_o(0, 1)
-    qkv_far(3)
-    wo_load.wait()
-    project_o(0)
-    relay_o(1, 0)
-    attention(2)
-    relay_o(1, 1)
-    qkv_near(3)
+    qkv_send(3)
+    relay_o(0)
+    qkv_take(3, 1)
     for j in range(n_full + 1):
         for nh in range(2):
             down_load(j, nh, FW if j < n_full else last_w).start()
+    wo_load.wait()
+    project_o(0)
+    attention(2)
+    relay_o(1)
     project_o(1)
     residual(0)
     attention(3)
-    relay_o(2, 0)
-    relay_o(2, 1)
     norm2(0)
+    gu_loop(0, 0, 1)
+    relay_o(2)
+    gu_add(0, 0, FW)
     project_o(2)
-    gu_loop(0, 0, 1)
-    relay_o(3, 0)
-    relay_o(3, 1)
     residual(1)
+    gu_loop(0, 1, 3, 1, 1)
+    relay_o(3)
+    gu_add(0, 2, FW)
+    norm2(1)
     project_o(3)
-    gu_loop(0, 1, 5)
-    norm2(1)
+    gu_loop(0, 3, 5, 2, 3)
+    gu_last(0)
     residual(2)
-    gu_last(0)
     gu_loop(1, 0, 1)
     gu_flush(0)
+    gu_loop(1, 1, 3)
     residual(3)
-    gu_loop(1, 1, 5)
     norm2(2)
+    gu_loop(1, 3, 5)
     gu_last(1)
-    gu_loop(2, 0, 1)
     gu_flush(1)
-    gu_loop(2, 1, 5)
+    act_all(0)
+    gu_loop(2, 0, 3)
     norm2(3)
+    gu_loop(2, 3, 5)
     gu_last(2)
-    gu_loop(3, 0, 1)
     gu_flush(2)
-    gu_loop(3, 1, 5)
+    act_all(1)
+    gu_loop(3, 0, 5)
     gu_last(3)
     gu_flush(3)
-    act_all(0)
-    act_all(1)
+    relay_all(0)
     down_all(0, 2)
+    relay_all(1)
     down_all(1, 3)
-    down_all(2, None)
-    down_all(3, None)
+    relay_down(2)
+    relay_down(3)
     stores = []
     for h in range(NCH):
         cp = store_out(h)
@@ -483,8 +527,7 @@
             d_copy(h, 1, m).wait_send()
             x_copy(h, m).wait_send()
             s2_copy(h, m + 1).wait_send()
-            for k in range(2):
-                o_copy(h, m, k).wait_send()
+            o_copy(h, m).wait_send()
         for nh in range(2):
             p_copy(h, nh).wait_send()
         for j in range(n_full + 1):
@@ -545,7 +588,7 @@
                 vm((8, 8, 128), F32),
                 vm((NCH, 4, 8, 128), F32),
                 dma((NCH + 2,)), dma((48,)),
-                *(dma((n,)) for n in (NCH, 8, 6 * NCH, 3 * NCH, 6 * NCH, 2 * NCH, 4 * NCH, 6 * NCH, 6 * NCH, 18 * NCH, NCH) for _ in range(2)),
+                *(dma((n,)) for n in (NCH, 8, 6 * NCH, 3 * NCH, 3 * NCH, 2 * NCH, 4 * NCH, 6 * NCH, 6 * NCH, 18 * NCH, NCH) for _ in range(2)),
             ],
             compiler_params=pltpu.CompilerParams(collective_id=0, has_side_effects=True, vmem_limit_bytes=67043328),
             name="layer",

time: 112 us -> 102 us (0.911)
  Pallas kernels: 111 us -> 100 us
    pallas_call x1, Pallas kernels: 111 us -> 100 us  [layer_fn(): pl.pallas_call(layer_kernel, out_shape=jax.ShapeDtypeStruct(x_blk.shape,...]
where the time goes in v4:
time: 102 us
  Pallas kernels  100 us (98%)
  local copies, waits for them, and re-layouts  1.67 us (2%)
    pallas_call x1, Pallas kernels, layer_fn(): pl.pallas_call(layer_kernel, out_shape=jax.ShapeDtypeStruct(x_blk.shape,...  100 us

profile of v4, /device:TPU:0, one launch (start us, length us, event | category | flops | bytes accessed | tf_op | source)
XLA Modules:
  0.0 101.8 jit_solution(6690870382252179309)
XLA Ops:
  0.0 100.1 %layer.1 = bf16[1,128,1024]{2,1,0:T(8,128)(2,1)} custom-call(bf16[1,128,1024]{2,1,0:T(8,128)(2,1)} %x_hbm.1, bf16[1024,2048]{1,0:T(8,128)(2,1)} %wq_hbm.1, bf16[1024,2048]{1,0:T(8,128)(2,1)} %wk_hbm.1, bf16[1024,2048]{1,0:T(8,128)(2,1)} %wv_hbm.1, bf16[2048,1024]{1,0:T(8,128)(2,1)} %wo_hbm.1, bf16[1024,5504]{1,0:T(8,128)(2,1)} %wg_hbm.1, ...), custom_call_target="tpu_custom_call" | custom-call | tf_op jit(solution)/shard_map/layer/pallas_call | solution.py:556
  100.1 1.7 %copy.12 = bf16[1,128,1024]{2,1,0:T(8,128)(2,1)} copy(bf16[1,128,1024]{2,1,0:T(8,128)(2,1)} %layer.1) | data formatting | bytes 524288

commit v5 on v4

--- a/solution.py
+++ b/solution.py
@@ -19,6 +19,26 @@
 ROWS = 2 * TOK
 SUB = ROWS // 4
 FW = 1024
+
+PIECES = ((1024, 2048, 2432), (3072, 2432), (3072, 2432), (2048, 2048, 1408))
+ORDER = (
+    ('qa', 0, 0), ('qb', 0, 0), ('qc', 0, 0), ('qa', 1, 0), ('qs', 0, 0), ('qb', 1, 0),
+    ('qs', 1, 0), ('at', 0, 0), ('qc', 1, 0), ('qa', 2, 0), ('qb', 2, 0), ('qs', 2, 0),
+    ('qc', 2, 0), ('qa', 3, 0), ('at', 1, 0), ('qb', 3, 0), ('qs', 3, 0), ('ro', 0, 0),
+    ('pr', 0, 0), ('ro', 1, 0), ('re', 0, 0), ('pr', 1, 0), ('at', 2, 0), ('qc', 3, 0),
+    ('at', 3, 0), ('n2', 0, 0), ('gm', 0, 0), ('gm', 0, 1), ('ro', 2, 0), ('ga', 0, 0),
+    ('re', 1, 0), ('ga', 0, 1), ('gm', 0, 2), ('pr', 2, 0), ('n2', 1, 0), ('ro', 3, 0),
+    ('ac', 0, 0), ('ga', 0, 2), ('gm', 1, 0), ('gm', 1, 1), ('ga', 1, 0), ('re', 2, 0),
+    ('ga', 1, 1), ('pr', 3, 0), ('ac', 1, 0), ('n2', 2, 0), ('re', 3, 0), ('ac', 0, 2),
+    ('ac', 0, 1), ('gm', 2, 0), ('n2', 3, 0), ('ga', 2, 0), ('ac', 1, 1), ('gm', 2, 1),
+    ('gm', 3, 0), ('ra', 0, 1), ('ra', 0, 0), ('ga', 3, 0), ('ga', 2, 1), ('ac', 2, 0),
+    ('ra', 1, 0), ('dn', 1, 0), ('dn', 0, 0), ('gm', 3, 1), ('ra', 1, 1), ('ga', 3, 1),
+    ('gm', 3, 2), ('ra', 0, 2), ('dn', 1, 1), ('ga', 3, 2), ('fi', 1, 0), ('ac', 3, 0),
+    ('ra', 2, 0), ('ac', 2, 1), ('dn', 0, 1), ('dn', 0, 2), ('ac', 3, 1), ('ac', 3, 2),
+    ('dn', 2, 0), ('fi', 0, 0), ('ra', 3, 0), ('ra', 2, 1), ('dn', 3, 0), ('ra', 3, 1),
+    ('dn', 2, 1), ('ra', 3, 2), ('fi', 2, 0), ('dn', 3, 1), ('dn', 3, 2), ('fi', 3, 0),
+    ('ou', 1, 0), ('ou', 0, 0), ('ou', 2, 0), ('ou', 3, 0),
+)
 
 
 def dot(a, b):
@@ -94,13 +114,16 @@
     def seq_rows(s):
         return pl.ds(pl.multiple_of(s * TOK, TOK), TOK)
 
-    def d_copy(h, z, m):
-        i = (h * 2 + z) * 3 + m
-        return remote(d_send.at[i], d_recv.at[i], d_s.at[i], d_r.at[i], core_peer)
-
-    def x_copy(h, m):
-        i = h * 3 + m
-        return remote(d_recv.at[h * 6 + m], x_recv.at[i], x_s.at[i], x_r.at[i], x_peer)
+    def d_copy(h, z, m=None):
+        i = (h * 2 + z) * 3 + (0 if m is None else m)
+        sl = pl.ds(i, 3) if m is None else i
+        return remote(d_send.at[sl], d_recv.at[sl], d_s.at[i], d_r.at[i], core_peer)
+
+    def x_copy(h, m=None):
+        i = h * 3 + (0 if m is None else m)
+        k = h * 6 + (0 if m is None else m)
+        src, dst = (d_recv.at[pl.ds(k, 3)], x_recv.at[pl.ds(i, 3)]) if m is None else (d_recv.at[k], x_recv.at[i])
+        return remote(src, dst, x_s.at[i], x_r.at[i], x_peer)
 
     def o_copy(h, kind):
         slot = (t, t, rel[2])[kind]
@@ -116,20 +139,26 @@
         i = h * 4 + k
         return remote(st2.at[h, 0], st2.at[h, k], s2_s.at[i], s2_r.at[i], peer[k])
 
-    def g_copy(h, j, w):
-        i = h * 6 + j
-        return remote(g_send.at[i, :, :, pl.ds(0, w)], g_recv.at[i, :, :, pl.ds(0, w)], g_s.at[i], g_r.at[i], core_peer)
-
-    def gx_copy(h, j, w):
-        i = h * 6 + j
-        return remote(g_recv.at[i, :, pl.ds(0, SUB), pl.ds(0, w)], gx_recv.at[i, :, :, pl.ds(0, w)], gx_s.at[i], gx_r.at[i], x_peer)
-
-    def a_copy(h, j, w, kind):
+    def piece(h, j):
+        start = sum(PIECES[h][:j])
+        return start, PIECES[h][j]
+
+    def g_copy(h, j):
+        cl = pl.ds(*piece(h, j))
+        i = h * 4 + j
+        return remote(g_send.at[h, :, :, cl], g_recv.at[h, :, :, cl], g_s.at[i], g_r.at[i], core_peer)
+
+    def gx_copy(h, j):
+        cl = pl.ds(*piece(h, j))
+        i = h * 4 + j
+        return remote(g_recv.at[h, :, pl.ds(0, SUB), cl], gx_recv.at[h, :, :, cl], gx_s.at[i], gx_r.at[i], x_peer)
+
+    def a_copy(h, j, kind):
         own = c * 2 + xc
         slot = (own, own, c * 2 + 1 - xc)[kind]
-        i = h * 6 + j
-        ref = a_all.at[i, slot, :, pl.ds(0, w)]
-        return remote(ref, ref, a_s.at[i * 3 + kind], a_r.at[i * 3 + kind], (core_peer, x_peer, core_peer)[kind])
+        i = (h * 4 + j) * 3 + kind
+        ref = a_all.at[h, slot, :, pl.ds(*piece(h, j))]
+        return remote(ref, ref, a_s.at[i], a_r.at[i], (core_peer, x_peer, core_peer)[kind])
 
     def f_copy(h):
         return remote(f_send.at[h], f_recv.at[h], f_s.at[h], f_r.at[h], y_peer)
@@ -184,69 +213,84 @@
         n = ((x_own(h, s) - mean[sl]) * rstd[sl]).astype(BF)
         n_buf[h, pl.ds(pl.multiple_of(s * TOK, TOK), TOK)] = n
 
-    def qkv_block(h, r, after):
-        def body(m, carry):
-            if h == 0:
-                qkv_wait(r, m)
-            after(m, dot(n_buf[h], wbuf[r * 3 + m]))
-            return carry
-
-        lax.fori_loop(0, 3, body, 0)
-
-    def give(h, z):
-        def after(m, res):
-            d_send[(h * 2 + z) * 3 + m] = res.astype(BF)
-            d_copy(h, z, m).start()
-        return after
-
-    def take(h, z):
-        def after(m, res):
-            d_copy(h, z, m).wait_recv()
-            i = (h * 2 + z) * 3 + m
-            d_recv[i] = (res + d_recv[i].astype(F32)).astype(BF)
-            if z == 0:
-                x_copy(h, m).start()
-        return after
-
     def norm_chunk(h):
         norm_rows(h, y, mean_o, rstd_o)
         xy_copy(h).wait_recv()
         norm_rows(h, 1 - y, mean_p, rstd_p)
 
-    def qkv_first():
-        norm_chunk(0)
-        qkv_block(0, 3, give(0, 0))
-        qkv_block(0, 2, take(0, 0))
-        qkv_block(0, 1, give(0, 1))
-        qkv_block(0, 0, take(0, 1))
-
-    def qkv_give(h):
-        norm_chunk(h)
-        for z in range(2):
-            for m in range(3):
-                d_send[(h * 2 + z) * 3 + m] = dot(n_buf[h], wbuf[(3 - 2 * z) * 3 + m]).astype(BF)
-            for m in range(3):
-                d_copy(h, z, m).start()
+    def qkv_give(h, z):
+        for m in range(3):
+            d_send[(h * 2 + z) * 3 + m] = dot(n_buf[h], wbuf[(3 - 2 * z) * 3 + m]).astype(BF)
+        d_copy(h, z).start()
 
     def qkv_take(h, z):
         own = [dot(n_buf[h], wbuf[(2 - 2 * z) * 3 + m]) for m in range(3)]
-        for m in range(3):
-            d_copy(h, z, m).wait_recv()
+        d_copy(h, z).wait_recv()
         for m in range(3):
             i = (h * 2 + z) * 3 + m
             d_recv[i] = (own[m] + d_recv[i].astype(F32)).astype(BF)
 
-    def qkv_send(h):
+    def step_qa(h, _):
+        norm_chunk(h)
+        if h > 0:
+            qkv_give(h, 0)
+            qkv_give(h, 1)
+            return
+
+        def body(m, carry):
+            qkv_wait(3, m)
+            d_send[m] = dot(n_buf[0], wbuf[9 + m]).astype(BF)
+            d_copy(0, 0, m).start()
+            return carry
+
+        lax.fori_loop(0, 3, body, 0)
+
+    def step_qb(h, _):
+        if h > 0:
+            qkv_take(h, 0)
+            return
+
+        def body(m, carry):
+            qkv_wait(2, m)
+            own = dot(n_buf[0], wbuf[6 + m])
+            d_copy(0, 0, m).wait_recv()
+            d_recv[m] = (own + d_recv[m].astype(F32)).astype(BF)
+            x_copy(0, m).start()
+            return carry
+
+        lax.fori_loop(0, 3, body, 0)
         for m in range(3):
-            x_copy(h, m).start()
+            qkv_wait(1, m)
+        qkv_give(0, 1)
+
+    def step_qs(h, _):
+        if h > 0:
+            x_copy(h).start()
+
+    def step_qc(h, _):
+        if h == 0:
+            for m in range(3):
+                qkv_wait(0, m)
+        qkv_take(h, 1)
+        if h == 0:
+            for j in range(n_full + 1):
+                for i in range(2):
+                    gu_load(i, j, FW if j < n_full else last_w).start()
+        if h == NCH - 1:
+            for j in range(n_full + 1):
+                for nh in range(2):
+                    down_load(j, nh, FW if j < n_full else last_w).start()
 
     def rotate(v, cos2, sin2):
         f = v.astype(F32)
         return (f * cos2 + pltpu.roll(f, HEAD_DIM // 2, 1) * sin2).astype(BF)
 
-    def attention(h):
-        for m in range(3):
+    def step_at(h, _):
+        for m in range(3) if h == 0 else (None,):
             x_copy(h, m).wait_recv()
+        if h == 0:
+            for tb in tables:
+                tb.wait()
 
         def final(m):
             return (d_recv[h * 6 + 3 + m].astype(F32) + x_recv[h * 3 + m].astype(F32)).astype(BF)
@@ -278,11 +322,13 @@
         o_copy(h, 1).start()
         o_copy(h, 0).start()
 
-    def relay_o(h):
+    def step_ro(h, _):
         o_copy(h, 1).wait_recv()
         o_copy(h, 2).start()
 
-    def project_o(h):
+    def step_pr(h, _):
+        if first_time("wo"):
+            wo_load.wait()
         o_copy(h, 0).wait_recv()
         o_copy(h, 2).wait_recv()
         for nh in range(2):
@@ -293,7 +339,7 @@
             p_send[h, :, cl] = res.astype(BF)
             p_copy(h, nh).start()
 
-    def residual(h):
+    def step_re(h, _):
         for nh in range(2):
             p_copy(h, nh).wait_recv()
         attn = (p_send[h].astype(F32) + p_recv[h].astype(F32)).astype(BF).astype(F32)
@@ -304,7 +350,7 @@
         for k in range(1, 4):
             s2_copy(h, k).start()
 
-    def norm2(h):
+    def step_n2(h, _):
         for k in range(1, 4):
             s2_copy(h, k).wait_recv()
         mean, rstd = moments((st2[h, 0] + st2[h, 1]) + (st2[h, 2] + st2[h, 3]))
@@ -314,124 +360,95 @@
             e_x = xc if b % 2 == 1 else 1 - xc
             n_buf[h, pl.ds(pl.multiple_of(2 * SUB * e_c + SUB * e_x, SUB), SUB)] = n[b * SUB:(b + 1) * SUB]
 
-    def gu_mul(h, j, w):
-        slot = (h * 6 + j) % 4 if isinstance(j, int) else lax.rem(h * 6 + j, 4)
-        if h == 0:
-            for i in range(2):
-                gu_load(i, j, w).wait()
-        for i, wv in enumerate((wg_v, wu_v)):
-            for n0 in range(0, w, 512):
-                nw = min(512, w - n0)
-                start = j * FW + n0 if isinstance(j, int) else pl.multiple_of(j * FW + n0, 512)
-                res = dot(n_buf[h], wv[:, pl.ds(start, nw)])
-                g_send[h * 6 + j, i, :, n0:n0 + nw] = res[0:2 * SUB].astype(BF)
-                g_own[slot, i, :, n0:n0 + nw] = res[2 * SUB:ROWS]
-        g_copy(h, j, w).start()
-
-    def gu_add(h, j, w):
-        slot = (h * 6 + j) % 4 if isinstance(j, int) else lax.rem(h * 6 + j, 4)
-        g_copy(h, j, w).wait_recv()
-        i = h * 6 + j
+    def steps(h, j, body):
+        start, w = piece(h, j)
+        lo, n = start // FW, w // FW
+        if n == 1:
+            body(lo, FW)
+        elif n > 1:
+            def step(kb, carry):
+                body(kb, FW)
+                return carry
+
+            lax.fori_loop(lo, lo + n, step, 0)
+        if w % FW:
+            body(lo + n, w % FW)
+
+    def step_gm(h, j):
+        if first_time("gu"):
+            for kb in range(n_full + 1):
+                for i in range(2):
+                    gu_load(i, kb, FW if kb < n_full else last_w).wait()
+        slot = own_slot[h, j]
+        start = piece(h, j)[0]
+
+        def body(kb, w):
+            for i, wv in enumerate((wg_v, wu_v)):
+                for n0 in range(0, w, 512):
+                    nw = min(512, w - n0)
+                    col = kb * FW + n0
+                    if not isinstance(col, int):
+                        col = pl.multiple_of(col, 512)
+                    res = dot(n_buf[h], wv[:, pl.ds(col, nw)])
+                    g_send[h, i, :, pl.ds(col, nw)] = res[0:2 * SUB].astype(BF)
+                    g_own[slot, i, :, pl.ds(col - start, nw)] = res[2 * SUB:ROWS]
+
+        steps(h, j, body)
+        g_copy(h, j).start()
+
+    def step_ga(h, j):
+        slot = own_slot[h, j]
+        start, w = piece(h, j)
+        cl = slice(start, start + w)
+        g_copy(h, j).wait_recv()
         for k in range(2):
-            g_recv[i, k, :, 0:w] = (g_own[slot, k, :, 0:w] + g_recv[i, k, :, 0:w].astype(F32)).astype(BF)
-        gx_copy(h, j, w).start()
-
-    def gu_loop(h, j0, j1, lag=2, first=0):
-        def body(j, carry):
-            gu_mul(h, j, FW)
-
-            @pl.when(j >= lag + first)
-            def _():
-                gu_add(h, j - lag, FW)
-            return carry
-
-        if j1 - j0 == 1 and j0 < lag + first:
-            gu_mul(h, j0, FW)
-        else:
-            lax.fori_loop(j0, j1, body, 0)
-
-    def gu_last(h):
-        gu_mul(h, n_full, last_w)
-        gu_add(h, n_full - 2, FW)
-
-    def gu_flush(h):
-        gu_add(h, n_full - 1, FW)
-        gu_add(h, n_full, last_w)
-
-    def act(h, j, w):
-        gx_copy(h, j, w).wait_recv()
-        i = h * 6 + j
+            g_recv[h, k, :, cl] = (g_own[slot, k, :, 0:w] + g_recv[h, k, :, cl].astype(F32)).astype(BF)
+        gx_copy(h, j).start()
+
+    def step_ac(h, j):
+        start, w = piece(h, j)
+        cl = slice(start, start + w)
+        gx_copy(h, j).wait_recv()
         g, u = [
-            (g_recv[i, k, SUB:2 * SUB, 0:w].astype(F32) + gx_recv[i, k, :, 0:w].astype(F32)).astype(BF).astype(F32)
+            (g_recv[h, k, SUB:2 * SUB, cl].astype(F32) + gx_recv[h, k, :, cl].astype(F32)).astype(BF).astype(F32)
             for k in range(2)
         ]
-        a_all[i, c * 2 + xc, :, 0:w] = (g * (1.0 / (1.0 + jnp.exp(-g))) * u).astype(BF)
-        a_copy(h, j, w, 1).start()
-        a_copy(h, j, w, 0).start()
-
-    def relay_a(h, j, w):
-        a_copy(h, j, w, 1).wait_recv()
-        a_copy(h, j, w, 2).start()
-
-    def down(h, j, w):
-        a_copy(h, j, w, 0).wait_recv()
-        a_copy(h, j, w, 2).wait_recv()
-        if h == 0:
+        a_all[h, c * 2 + xc, :, cl] = (g * (1.0 / (1.0 + jnp.exp(-g))) * u).astype(BF)
+        a_copy(h, j, 1).start()
+        a_copy(h, j, 0).start()
+
+    def step_ra(h, j):
+        a_copy(h, j, 1).wait_recv()
+        a_copy(h, j, 2).start()
+
+    def step_dn(h, j):
+        if first_time("down"):
+            for kb in range(n_full + 1):
+                for nh in range(2):
+                    down_load(kb, nh, FW if kb < n_full else last_w).wait()
+        a_copy(h, j, 0).wait_recv()
+        a_copy(h, j, 2).wait_recv()
+        if j == 0:
+            acc[h] = jnp.zeros((ROWS, width), F32)
+
+        def body(kb, w):
+            col = kb * FW if isinstance(kb, int) else pl.multiple_of(kb * FW, FW)
+            lhs = a_all[h, :, :, pl.ds(col, w)].reshape(ROWS, w)
             for nh in range(2):
-                down_load(j, nh, w).wait()
-        lhs = a_all[h * 6 + j, :, :, 0:w].reshape(ROWS, w)
-        for nh in range(2):
-            acc[h, :, nh * 512:(nh + 1) * 512] += dot(lhs, wbuf[j * 2 + nh, 0:w])
-
-    def act_all(h):
-        def body(j, carry):
-            act(h, j, FW)
-            return carry
-
-        lax.fori_loop(0, n_full, body, 0)
-        act(h, n_full, last_w)
-
-    def relay_all(h):
-        def body(j, carry):
-            relay_a(h, j, FW)
-            return carry
-
-        lax.fori_loop(0, n_full, body, 0)
-        relay_a(h, n_full, last_w)
-
-    def down_all(h, beside):
-        acc[h] = jnp.zeros((ROWS, width), F32)
-
-        def body(j, carry):
-            act(beside, j, FW)
-            down(h, j, FW)
-            return carry
-
-        lax.fori_loop(0, n_full, body, 0)
-        act(beside, n_full, last_w)
-        down(h, n_full, last_w)
-        down_send(h)
-
-    def down_send(h):
+                acc[h, :, nh * 512:(nh + 1) * 512] += dot(lhs, wbuf[kb * 2 + nh, 0:w])
+
+        steps(h, j, body)
+
+    def step_fi(h, _):
         f_send[h] = acc[h, seq_rows(1 - y)].astype(BF)
         f_copy(h).start()
 
-    def relay_down(h):
-        acc[h] = jnp.zeros((ROWS, width), F32)
-        relay_a(h, 0, FW)
-        relay_a(h, 1, FW)
-
-        def body(j, carry):
-            relay_a(h, j, FW)
-            down(h, j - 2, FW)
-            return carry
-
-        lax.fori_loop(2, n_full, body, 0)
-        relay_a(h, n_full, last_w)
-        down(h, n_full - 2, FW)
-        down(h, n_full - 1, FW)
-        down(h, n_full, last_w)
-        down_send(h)
+    stores = []
+
+    def step_ou(h, _):
+        cp = store_out(h)
+        cp.start()
+        stores.append(cp)
 
     def store_out(h):
         own = pl.ds(pl.multiple_of(y * TOK, TOK), TOK)
@@ -443,99 +460,42 @@
     for k in range(4, 8):
         s1_copy(k).wait_recv()
     mean_p, rstd_p = moments((st1[4] + st1[5]) + (st1[6] + st1[7]))
-    qkv_first()
-    for j in range(n_full + 1):
-        for i in range(2):
-            gu_load(i, j, FW if j < n_full else last_w).start()
-    qkv_give(1)
-    qkv_take(1, 0)
-    qkv_send(1)
-    qkv_take(1, 1)
-    for tb in tables:
-        tb.wait()
-    qkv_give(2)
-    qkv_take(2, 0)
-    attention(0)
-    qkv_send(2)
-    qkv_take(2, 1)
-    qkv_give(3)
-    qkv_take(3, 0)
-    attention(1)
-    qkv_send(3)
-    relay_o(0)
-    qkv_take(3, 1)
-    for j in range(n_full + 1):
-        for nh in range(2):
-            down_load(j, nh, FW if j < n_full else last_w).start()
-    wo_load.wait()
-    project_o(0)
-    attention(2)
-    relay_o(1)
-    project_o(1)
-    residual(0)
-    attention(3)
-    norm2(0)
-    gu_loop(0, 0, 1)
-    relay_o(2)
-    gu_add(0, 0, FW)
-    project_o(2)
-    residual(1)
-    gu_loop(0, 1, 3, 1, 1)
-    relay_o(3)
-    gu_add(0, 2, FW)
-    norm2(1)
-    project_o(3)
-    gu_loop(0, 3, 5, 2, 3)
-    gu_last(0)
-    residual(2)
-    gu_loop(1, 0, 1)
-    gu_flush(0)
-    gu_loop(1, 1, 3)
-    residual(3)
-    norm2(2)
-    gu_loop(1, 3, 5)
-    gu_last(1)
-    gu_flush(1)
-    act_all(0)
-    gu_loop(2, 0, 3)
-    norm2(3)
-    gu_loop(2, 3, 5)
-    gu_last(2)
-    gu_flush(2)
-    act_all(1)
-    gu_loop(3, 0, 5)
-    gu_last(3)
-    gu_flush(3)
-    relay_all(0)
-    down_all(0, 2)
-    relay_all(1)
-    down_all(1, 3)
-    relay_down(2)
-    relay_down(3)
-    stores = []
-    for h in range(NCH):
-        cp = store_out(h)
-        cp.start()
-        stores.append(cp)
+    seen = set()
+
+    def first_time(name):
+        new = name not in seen
+        seen.add(name)
+        return new
+
+    own_slot, free = {}, list(range(g_own.shape[0]))
+    for name, h, j in ORDER:
+        if name == "gm":
+            own_slot[h, j] = free.pop(0)
+        if name == "ga":
+            free.append(own_slot[h, j])
+    step_of = dict(qa=step_qa, qb=step_qb, qs=step_qs, qc=step_qc, at=step_at, ro=step_ro, pr=step_pr, re=step_re, n2=step_n2,
+                   gm=step_gm, ga=step_ga, ac=step_ac, ra=step_ra, dn=step_dn, fi=step_fi, ou=step_ou)
+    for name, h, j in ORDER:
+        step_of[name](h, j)
 
     for k in range(1, 8):
         s1_copy(k).wait_send()
     for h in range(NCH):
         xy_copy(h).wait_send()
+        for m in range(3) if h == 0 else (None,):
+            d_copy(h, 0, m).wait_send()
+            x_copy(h, m).wait_send()
+        d_copy(h, 1).wait_send()
         for m in range(3):
-            d_copy(h, 0, m).wait_send()
-            d_copy(h, 1, m).wait_send()
-            x_copy(h, m).wait_send()
             s2_copy(h, m + 1).wait_send()
             o_copy(h, m).wait_send()
         for nh in range(2):
             p_copy(h, nh).wait_send()
-        for j in range(n_full + 1):
-            w = FW if j < n_full else last_w
-            g_copy(h, j, w).wait_send()
-            gx_copy(h, j, w).wait_send()
+        for j in range(len(PIECES[h])):
+            g_copy(h, j).wait_send()
+            gx_copy(h, j).wait_send()
             for kind in range(3):
-                a_copy(h, j, w, kind).wait_send()
+                a_copy(h, j, kind).wait_send()
         f_copy(h).wait_send()
     for cp in stores:
         cp.wait()
@@ -576,11 +536,11 @@
                 vm((NCH, ROWS, width), BF),
                 vm((NCH, ROWS, width), BF),
                 vm((NCH, ROWS, width), BF),
-                vm((6 * NCH, 2, 2 * SUB, FW), BF),
-                vm((6 * NCH, 2, 2 * SUB, FW), BF),
-                vm((4, 2, 2 * SUB, FW), F32),
-                vm((6 * NCH, 2, SUB, FW), BF),
-                vm((6 * NCH, 4, SUB, FW), BF),
+                vm((NCH, 2, 2 * SUB, ff), BF),
+                vm((NCH, 2, 2 * SUB, ff), BF),
+                vm((3, 2, 2 * SUB, max(max(p) for p in PIECES)), F32),
+                vm((NCH, 2, SUB, ff), BF),
+                vm((NCH, 4, SUB, ff), BF),
                 vm((NCH, ROWS, width), F32),
                 vm((NCH, TOK, width), BF),
                 vm((NCH, TOK, width), BF),
@@ -588,7 +548,7 @@
                 vm((8, 8, 128), F32),
                 vm((NCH, 4, 8, 128), F32),
                 dma((NCH + 2,)), dma((48,)),
-                *(dma((n,)) for n in (NCH, 8, 6 * NCH, 3 * NCH, 3 * NCH, 2 * NCH, 4 * NCH, 6 * NCH, 6 * NCH, 18 * NCH, NCH) for _ in range(2)),
+                *(dma((n,)) for n in (NCH, 8, 6 * NCH, 3 * NCH, 3 * NCH, 2 * NCH, 4 * NCH, 4 * NCH, 4 * NCH, 12 * NCH, NCH) for _ in range(2)),
             ],
             compiler_params=pltpu.CompilerParams(collective_id=0, has_side_effects=True, vmem_limit_bytes=67043328),
             name="layer",

time: 102 us -> 99.3 us (0.974)
  Pallas kernels: 100 us -> 97.5 us
    pallas_call x1, Pallas kernels: 100 us -> 97.5 us  [layer_fn(): pl.pallas_call(layer_kernel, out_shape=jax.ShapeDtypeStruct(x_blk.shape,...]
where the time goes in v5:
time: 99.3 us; the launch traced here: 99.2 us
  Pallas kernels  97.5 us (98%)
  local copies, waits for them, and re-layouts  1.67 us (2%)
    pallas_call x1, Pallas kernels, layer_fn(): pl.pallas_call(layer_kernel, out_shape=jax.ShapeDtypeStruct(x_blk.shape,...  97.5 us

profile of v5, /device:TPU:0, one launch (start us, length us, event | category | flops | bytes accessed | tf_op | source)
XLA Modules:
  0.0 99.2 jit_solution(5927524891245735253)
XLA Ops:
  0.0 97.5 %layer.1 = bf16[1,128,1024]{2,1,0:T(8,128)(2,1)} custom-call(bf16[1,128,1024]{2,1,0:T(8,128)(2,1)} %x_hbm.1, bf16[1024,2048]{1,0:T(8,128)(2,1)} %wq_hbm.1, bf16[1024,2048]{1,0:T(8,128)(2,1)} %wk_hbm.1, bf16[1024,2048]{1,0:T(8,128)(2,1)} %wv_hbm.1, bf16[2048,1024]{1,0:T(8,128)(2,1)} %wo_hbm.1, bf16[1024,5504]{1,0:T(8,128)(2,1)} %wg_hbm.1, ...), custom_call_target="tpu_custom_call" | custom-call | tf_op jit(solution)/shard_map/layer/pallas_call | solution.py:516
  97.5 1.7 %copy.12 = bf16[1,128,1024]{2,1,0:T(8,128)(2,1)} copy(bf16[1,128,1024]{2,1,0:T(8,128)(2,1)} %layer.1) | data formatting | bytes 524288

commit v6 on v5

--- a/solution.py
+++ b/solution.py
@@ -20,24 +20,15 @@
 SUB = ROWS // 4
 FW = 1024
 
-PIECES = ((1024, 2048, 2432), (3072, 2432), (3072, 2432), (2048, 2048, 1408))
+PIECES = ((1024, 2048, 2432), (2048, 2048, 1408), (3072, 2432), (2048, 2048, 1408))
 ORDER = (
-    ('qa', 0, 0), ('qb', 0, 0), ('qc', 0, 0), ('qa', 1, 0), ('qs', 0, 0), ('qb', 1, 0),
-    ('qs', 1, 0), ('at', 0, 0), ('qc', 1, 0), ('qa', 2, 0), ('qb', 2, 0), ('qs', 2, 0),
-    ('qc', 2, 0), ('qa', 3, 0), ('at', 1, 0), ('qb', 3, 0), ('qs', 3, 0), ('ro', 0, 0),
-    ('pr', 0, 0), ('ro', 1, 0), ('re', 0, 0), ('pr', 1, 0), ('at', 2, 0), ('qc', 3, 0),
-    ('at', 3, 0), ('n2', 0, 0), ('gm', 0, 0), ('gm', 0, 1), ('ro', 2, 0), ('ga', 0, 0),
-    ('re', 1, 0), ('ga', 0, 1), ('gm', 0, 2), ('pr', 2, 0), ('n2', 1, 0), ('ro', 3, 0),
-    ('ac', 0, 0), ('ga', 0, 2), ('gm', 1, 0), ('gm', 1, 1), ('ga', 1, 0), ('re', 2, 0),
-    ('ga', 1, 1), ('pr', 3, 0), ('ac', 1, 0), ('n2', 2, 0), ('re', 3, 0), ('ac', 0, 2),
-    ('ac', 0, 1), ('gm', 2, 0), ('n2', 3, 0), ('ga', 2, 0), ('ac', 1, 1), ('gm', 2, 1),
-    ('gm', 3, 0), ('ra', 0, 1), ('ra', 0, 0), ('ga', 3, 0), ('ga', 2, 1), ('ac', 2, 0),
-    ('ra', 1, 0), ('dn', 1, 0), ('dn', 0, 0), ('gm', 3, 1), ('ra', 1, 1), ('ga', 3, 1),
-    ('gm', 3, 2), ('ra', 0, 2), ('dn', 1, 1), ('ga', 3, 2), ('fi', 1, 0), ('ac', 3, 0),
-    ('ra', 2, 0), ('ac', 2, 1), ('dn', 0, 1), ('dn', 0, 2), ('ac', 3, 1), ('ac', 3, 2),
-    ('dn', 2, 0), ('fi', 0, 0), ('ra', 3, 0), ('ra', 2, 1), ('dn', 3, 0), ('ra', 3, 1),
-    ('dn', 2, 1), ('ra', 3, 2), ('fi', 2, 0), ('dn', 3, 1), ('dn', 3, 2), ('fi', 3, 0),
-    ('ou', 1, 0), ('ou', 0, 0), ('ou', 2, 0), ('ou', 3, 0),
+    "qa0 qb0 qs0 qa1", "qb1 qs1 qc0 qa2", "at0 qb2 qc1 qs2", "qc2 qa3 ro0 at1",
+    "qb3 qs3 pr0 qc3", "ro1 pr1 re0 at2", "at3 n20 gm00 gm01", "ro2 ga00 re1 ga01",
+    "ro3 gm02 ac00 pr2", "ga02 pr3 n21 ac01", "gm10 re2 ga10 ac02", "gm11 ga11 gm12 ac10",
+    "re3 n22 ga12 gm20", "ac11 ra00 n23 ga20", "dn00 ra10 gm21 ga21", "gm30 ra01 ga30 ra02",
+    "ac20 gm31 ga31 gm32", "ac21 dn10 ga32 ac12", "ra20 dn01 dn02 dn20", "ra11 ra21 fi0 ac30",
+    "dn11 ac31 ac32 ra12", "dn21 fi2 ra30 ou0", "dn12 fi1 ra31 dn30", "ra32 dn31 dn32 fi3",
+    "ou1 ou2 ou3",
 )
 
 
@@ -114,16 +105,21 @@
     def seq_rows(s):
         return pl.ds(pl.multiple_of(s * TOK, TOK), TOK)
 
-    def d_copy(h, z, m=None):
+    def part_rows(part):
+        return seq_rows(y if part == 0 else 1 - y)
+
+    def d_copy(h, z, m=None, part=None):
         i = (h * 2 + z) * 3 + (0 if m is None else m)
-        sl = pl.ds(i, 3) if m is None else i
-        return remote(d_send.at[sl], d_recv.at[sl], d_s.at[i], d_r.at[i], core_peer)
-
-    def x_copy(h, m=None):
+        src, dst = (d_send.at[pl.ds(i, 3)], d_recv.at[pl.ds(i, 3)]) if m is None else (d_send.at[i, part_rows(part)], d_recv.at[i, part_rows(part)])
+        k = 6 * NCH + m if part == 1 else i
+        return remote(src, dst, d_s.at[k], d_r.at[k], core_peer)
+
+    def x_copy(h, m=None, part=None):
         i = h * 3 + (0 if m is None else m)
         k = h * 6 + (0 if m is None else m)
-        src, dst = (d_recv.at[pl.ds(k, 3)], x_recv.at[pl.ds(i, 3)]) if m is None else (d_recv.at[k], x_recv.at[i])
-        return remote(src, dst, x_s.at[i], x_r.at[i], x_peer)
+        src, dst = (d_recv.at[pl.ds(k, 3)], x_recv.at[pl.ds(i, 3)]) if m is None else (d_recv.at[k, part_rows(part)], x_recv.at[i, part_rows(part)])
+        n = 3 * NCH + m if part == 1 else i
+        return remote(src, dst, x_s.at[n], x_r.at[n], x_peer)
 
     def o_copy(h, kind):
         slot = (t, t, rel[2])[kind]
@@ -173,7 +169,7 @@
         m = jnp.where(lane[0:n] == 0, s, jnp.where(lane[0:n] == 1, q, 0.0))
         if n < 128:
             m = jnp.concatenate([m, jnp.zeros((128 - n, 128), F32)], axis=0)
-        return m.T[0:8]
+        return m.T[0:2]
 
     def moments(total):
         mean = total[0:1] / full_width
@@ -213,10 +209,12 @@
         n = ((x_own(h, s) - mean[sl]) * rstd[sl]).astype(BF)
         n_buf[h, pl.ds(pl.multiple_of(s * TOK, TOK), TOK)] = n
 
+    first_parts = [(m, part) for part in range(2) for m in range(3)]
+
     def norm_chunk(h):
         norm_rows(h, y, mean_o, rstd_o)
         xy_copy(h).wait_recv()
-        norm_rows(h, 1 - y, mean_p, rstd_p)
+        norm_rows(h, 1 - y, *other_moments)
 
     def qkv_give(h, z):
         for m in range(3):
@@ -230,35 +228,47 @@
             i = (h * 2 + z) * 3 + m
             d_recv[i] = (own[m] + d_recv[i].astype(F32)).astype(BF)
 
+    def qkv_part(part):
+        rows = part_rows(part)
+
+        def give(m, carry):
+            if part == 0:
+                qkv_wait(3, m)
+            d_send[m, rows] = dot(n_buf[0, rows], wbuf[9 + m]).astype(BF)
+            d_copy(0, 0, m, part).start()
+            return carry
+
+        def take(m, carry):
+            if part == 0:
+                qkv_wait(2, m)
+            own = dot(n_buf[0, rows], wbuf[6 + m])
+            d_copy(0, 0, m, part).wait_recv()
+            d_recv[m, rows] = (own + d_recv[m, rows].astype(F32)).astype(BF)
+            x_copy(0, m, part).start()
+            return carry
+
+        lax.fori_loop(0, 3, give, 0)
+        lax.fori_loop(0, 3, take, 0)
+
     def step_qa(h, _):
-        norm_chunk(h)
         if h > 0:
+            norm_chunk(h)
             qkv_give(h, 0)
             qkv_give(h, 1)
-            return
-
-        def body(m, carry):
-            qkv_wait(3, m)
-            d_send[m] = dot(n_buf[0], wbuf[9 + m]).astype(BF)
-            d_copy(0, 0, m).start()
-            return carry
-
-        lax.fori_loop(0, 3, body, 0)
+        else:
+            norm_rows(0, y, mean_o, rstd_o)
+            qkv_part(0)
 
     def step_qb(h, _):
         if h > 0:
             qkv_take(h, 0)
             return
-
-        def body(m, carry):
-            qkv_wait(2, m)
-            own = dot(n_buf[0], wbuf[6 + m])
-            d_copy(0, 0, m).wait_recv()
-            d_recv[m] = (own + d_recv[m].astype(F32)).astype(BF)
-            x_copy(0, m).start()
-            return carry
-
-        lax.fori_loop(0, 3, body, 0)
+        for k in range(4, 8):
+            s1_copy(k).wait_recv()
+        other_moments.extend(moments((st1[4] + st1[5]) + (st1[6] + st1[7])))
+        xy_copy(0).wait_recv()
+        norm_rows(0, 1 - y, *other_moments)
+        qkv_part(1)
         for m in range(3):
             qkv_wait(1, m)
         qkv_give(0, 1)
@@ -286,8 +296,8 @@
         return (f * cos2 + pltpu.roll(f, HEAD_DIM // 2, 1) * sin2).astype(BF)
 
     def step_at(h, _):
-        for m in range(3) if h == 0 else (None,):
-            x_copy(h, m).wait_recv()
+        for m, part in first_parts if h == 0 else ((None, None),):
+            x_copy(h, m, part).wait_recv()
         if h == 0:
             for tb in tables:
                 tb.wait()
@@ -457,9 +467,7 @@
         y_buf[h] = (h_buf[h, own].astype(F32) + mlp).astype(BF)
         return pltpu.make_async_copy(y_buf.at[h], out_hbm.at[0, pl.ds(h * TOK, TOK)], ld_sem.at[h])
 
-    for k in range(4, 8):
-        s1_copy(k).wait_recv()
-    mean_p, rstd_p = moments((st1[4] + st1[5]) + (st1[6] + st1[7]))
+    other_moments = []
     seen = set()
 
     def first_time(name):
@@ -468,23 +476,24 @@
         return new
 
     own_slot, free = {}, list(range(g_own.shape[0]))
-    for name, h, j in ORDER:
+    program = [(w[:2], int(w[2]), int(w[3:] or 0)) for line in ORDER for w in line.split()]
+    for name, h, j in program:
         if name == "gm":
             own_slot[h, j] = free.pop(0)
         if name == "ga":
             free.append(own_slot[h, j])
     step_of = dict(qa=step_qa, qb=step_qb, qs=step_qs, qc=step_qc, at=step_at, ro=step_ro, pr=step_pr, re=step_re, n2=step_n2,
                    gm=step_gm, ga=step_ga, ac=step_ac, ra=step_ra, dn=step_dn, fi=step_fi, ou=step_ou)
-    for name, h, j in ORDER:
+    for name, h, j in program:
         step_of[name](h, j)
 
     for k in range(1, 8):
         s1_copy(k).wait_send()
     for h in range(NCH):
         xy_copy(h).wait_send()
-        for m in range(3) if h == 0 else (None,):
-            d_copy(h, 0, m).wait_send()
-            x_copy(h, m).wait_send()
+        for m, part in first_parts if h == 0 else ((None, None),):
+            d_copy(h, 0, m, part).wait_send()
+            x_copy(h, m, part).wait_send()
         d_copy(h, 1).wait_send()
         for m in range(3):
             s2_copy(h, m + 1).wait_send()
@@ -545,10 +554,10 @@
                 vm((NCH, TOK, width), BF),
                 vm((NCH, TOK, width), BF),
                 vm((NCH, TOK, width), BF),
-                vm((8, 8, 128), F32),
-                vm((NCH, 4, 8, 128), F32),
+                vm((8, 2, 128), F32),
+                vm((NCH, 4, 2, 128), F32),
                 dma((NCH + 2,)), dma((48,)),
-                *(dma((n,)) for n in (NCH, 8, 6 * NCH, 3 * NCH, 3 * NCH, 2 * NCH, 4 * NCH, 4 * NCH, 4 * NCH, 12 * NCH, NCH) for _ in range(2)),
+                *(dma((n,)) for n in (NCH, 8, 6 * NCH + 3, 3 * NCH + 3, 3 * NCH, 2 * NCH, 4 * NCH, 4 * NCH, 4 * NCH, 12 * NCH, NCH) for _ in range(2)),
             ],
             compiler_params=pltpu.CompilerParams(collective_id=0, has_side_effects=True, vmem_limit_bytes=67043328),
             name="layer",

time: 99.3 us -> 97.2 us (0.979)
  Pallas kernels: 97.5 us -> 95.4 us
    pallas_call x1, Pallas kernels: 97.5 us -> 95.4 us  [layer_fn(): pl.pallas_call(layer_kernel, out_shape=jax.ShapeDtypeStruct(x_blk.shape,...]
where the time goes in v6:
time: 97.2 us; the launch traced here: 97 us
  Pallas kernels  95.4 us (98%)
  local copies, waits for them, and re-layouts  1.67 us (2%)
    pallas_call x1, Pallas kernels, layer_fn(): pl.pallas_call(layer_kernel, out_shape=jax.ShapeDtypeStruct(x_blk.shape,...  95.4 us

profile of v6, /device:TPU:0, one launch (start us, length us, event | category | flops | bytes accessed | tf_op | source)
XLA Modules:
  0.0 97.0 jit_solution(12822235773827947015)
XLA Ops:
  0.0 95.4 %layer.1 = bf16[1,128,1024]{2,1,0:T(8,128)(2,1)} custom-call(bf16[1,128,1024]{2,1,0:T(8,128)(2,1)} %x_hbm.1, bf16[1024,2048]{1,0:T(8,128)(2,1)} %wq_hbm.1, bf16[1024,2048]{1,0:T(8,128)(2,1)} %wk_hbm.1, bf16[1024,2048]{1,0:T(8,128)(2,1)} %wv_hbm.1, bf16[2048,1024]{1,0:T(8,128)(2,1)} %wo_hbm.1, bf16[1024,5504]{1,0:T(8,128)(2,1)} %wg_hbm.1, ...), custom_call_target="tpu_custom_call" | custom-call | tf_op jit(solution)/shard_map/layer/pallas_call | solution.py:525
  95.4 1.7 %copy.12 = bf16[1,128,1024]{2,1,0:T(8,128)(2,1)} copy(bf16[1,128,1024]{2,1,0:T(8,128)(2,1)} %layer.1) | data formatting | bytes 524288

commit v7 on v6

--- a/solution.py
+++ b/solution.py
@@ -49,9 +49,9 @@
     return np.concatenate([cos_t, cos_t], 1), np.concatenate([-sin_t, sin_t], 1)
 
 
-def layer_kernel(x_hbm, wq_hbm, wk_hbm, wv_hbm, wo_hbm, wg_hbm, wu_hbm, wd_hbm, cos_hbm, sin_hbm, out_hbm,
+def layer_kernel(x_hbm, wq_hbm, wk_hbm, wv_hbm, wo_hbm, wg_hbm, wu_hbm, wd_hbm, cos_hbm, sin_hbm, out_ref,
                  wbuf, wo_v, wg_v, wu_v, cos_v, sin_v, x_all, n_buf, d_send, d_recv, x_recv, k_buf, v_buf, o_all,
-                 p_send, p_recv, h_buf, g_send, g_recv, g_own, gx_recv, a_all, acc, f_send, f_recv, y_buf, st1, st2,
+                 p_send, p_recv, h_buf, g_send, g_recv, g_own, gx_recv, a_all, acc, f_send, f_recv, st1, st2,
                  ld_sem, w_sem, xy_s, xy_r, s1_s, s1_r, d_s, d_r, x_s, x_r, o_s, o_r, p_s, p_r, s2_s, s2_r,
                  g_s, g_r, gx_s, gx_r, a_s, a_r, f_s, f_r):
     dp = lax.axis_index("dp")
@@ -142,7 +142,7 @@
     def g_copy(h, j):
         cl = pl.ds(*piece(h, j))
         i = h * 4 + j
-        return remote(g_send.at[h, :, :, cl], g_recv.at[h, :, :, cl], g_s.at[i], g_r.at[i], core_peer)
+        return remote(g_send.at[h % 2, :, :, cl], g_recv.at[h, :, :, cl], g_s.at[i], g_r.at[i], core_peer)
 
     def gx_copy(h, j):
         cl = pl.ds(*piece(h, j))
@@ -389,6 +389,9 @@
             for kb in range(n_full + 1):
                 for i in range(2):
                     gu_load(i, kb, FW if kb < n_full else last_w).wait()
+        if h >= 2 and j == 0:
+            for k in range(len(PIECES[h - 2])):
+                g_copy(h - 2, k).wait_send()
         slot = own_slot[h, j]
         start = piece(h, j)[0]
 
@@ -400,7 +403,7 @@
                     if not isinstance(col, int):
                         col = pl.multiple_of(col, 512)
                     res = dot(n_buf[h], wv[:, pl.ds(col, nw)])
-                    g_send[h, i, :, pl.ds(col, nw)] = res[0:2 * SUB].astype(BF)
+                    g_send[h % 2, i, :, pl.ds(col, nw)] = res[0:2 * SUB].astype(BF)
                     g_own[slot, i, :, pl.ds(col - start, nw)] = res[2 * SUB:ROWS]
 
         steps(h, j, body)
@@ -453,19 +456,11 @@
         f_send[h] = acc[h, seq_rows(1 - y)].astype(BF)
         f_copy(h).start()
 
-    stores = []
-
     def step_ou(h, _):
-        cp = store_out(h)
-        cp.start()
-        stores.append(cp)
-
-    def store_out(h):
         own = pl.ds(pl.multiple_of(y * TOK, TOK), TOK)
         f_copy(h).wait_recv()
         mlp = (acc[h, own].astype(BF).astype(F32) + f_recv[h].astype(F32)).astype(BF).astype(F32)
-        y_buf[h] = (h_buf[h, own].astype(F32) + mlp).astype(BF)
-        return pltpu.make_async_copy(y_buf.at[h], out_hbm.at[0, pl.ds(h * TOK, TOK)], ld_sem.at[h])
+        out_ref[0, h * TOK:(h + 1) * TOK] = (h_buf[h, own].astype(F32) + mlp).astype(BF)
 
     other_moments = []
     seen = set()
@@ -501,13 +496,12 @@
         for nh in range(2):
             p_copy(h, nh).wait_send()
         for j in range(len(PIECES[h])):
-            g_copy(h, j).wait_send()
+            if h >= NCH - 2:
+                g_copy(h, j).wait_send()
             gx_copy(h, j).wait_send()
             for kind in range(3):
                 a_copy(h, j, kind).wait_send()
         f_copy(h).wait_send()
-    for cp in stores:
-        cp.wait()
 
 
 def solution(mesh):
@@ -524,9 +518,9 @@
         vm = pltpu.VMEM
         return pl.pallas_call(
             layer_kernel,
-            out_shape=jax.ShapeDtypeStruct(x_blk.shape, BF),
+            out_shape=pltpu.VMEM(x_blk.shape, BF),
             in_specs=[pl.BlockSpec(memory_space=pl.ANY)] * 10,
-            out_specs=pl.BlockSpec(memory_space=pl.ANY),
+            out_specs=pl.BlockSpec(memory_space=pltpu.VMEM),
             scratch_shapes=[
                 vm((12, width, cols), BF),
                 vm(w_o.shape, BF),
@@ -545,7 +539,7 @@
                 vm((NCH, ROWS, width), BF),
                 vm((NCH, ROWS, width), BF),
                 vm((NCH, ROWS, width), BF),
-                vm((NCH, 2, 2 * SUB, ff), BF),
+                vm((2, 2, 2 * SUB, ff), BF),
                 vm((NCH, 2, 2 * SUB, ff), BF),
                 vm((3, 2, 2 * SUB, max(max(p) for p in PIECES)), F32),
                 vm((NCH, 2, SUB, ff), BF),
@@ -553,13 +547,12 @@
                 vm((NCH, ROWS, width), F32),
                 vm((NCH, TOK, width), BF),
                 vm((NCH, TOK, width), BF),
-                vm((NCH, TOK, width), BF),
                 vm((8, 2, 128), F32),
                 vm((NCH, 4, 2, 128), F32),
                 dma((NCH + 2,)), dma((48,)),
                 *(dma((n,)) for n in (NCH, 8, 6 * NCH + 3, 3 * NCH + 3, 3 * NCH, 2 * NCH, 4 * NCH, 4 * NCH, 4 * NCH, 12 * NCH, NCH) for _ in range(2)),
             ],
-            compiler_params=pltpu.CompilerParams(collective_id=0, has_side_effects=True, vmem_limit_bytes=67043328),
+            compiler_params=pltpu.CompilerParams(collective_id=0, has_side_effects=True, vmem_limit_bytes=66256896),
             name="layer",
         )(x_blk, w_q, w_k, w_v, w_o, w_gate, w_up, w_down, cos_t, sin_t)
 

time: 97.2 us -> 95.7 us (0.985)
  no operation moved by 1% of the time
where the time goes in v7:
time: 95.7 us; the launch traced here: 95.6 us
  Pallas kernels  94.9 us (99%)
    pallas_call x1, Pallas kernels, layer_fn(): pl.pallas_call(layer_kernel, out_shape=pltpu.VMEM(x_blk.shape, BF), in_sp...  94.9 us

profile of v7, /device:TPU:0, one launch (start us, length us, event | category | flops | bytes accessed | tf_op | source)
XLA Modules:
  0.0 95.6 jit_solution(17995573423488691023)
XLA Ops:
  0.0 94.9 %layer.1 = bf16[1,128,1024]{2,1,0:T(8,128)(2,1)S(1)} custom-call(bf16[1,128,1024]{2,1,0:T(8,128)(2,1)} %x_hbm.1, bf16[1024,2048]{1,0:T(8,128)(2,1)} %wq_hbm.1, bf16[1024,2048]{1,0:T(8,128)(2,1)} %wk_hbm.1, bf16[1024,2048]{1,0:T(8,128)(2,1)} %wv_hbm.1, bf16[2048,1024]{1,0:T(8,128)(2,1)} %wo_hbm.1, bf16[1024,5504]{1,0:T(8,128)(2,1)} %wg_hbm.1, ...), custom_call_target="tpu_custom_call" | custom-call | tf_op jit(solution)/shard_map/layer/pallas_call | solution.py:519
  94.9 0.7 copy.12

commit v8 on v7

--- a/solution.py
+++ b/solution.py
@@ -22,13 +22,13 @@
 
 PIECES = ((1024, 2048, 2432), (2048, 2048, 1408), (3072, 2432), (2048, 2048, 1408))
 ORDER = (
-    "qa0 qb0 qs0 qa1", "qb1 qs1 qc0 qa2", "at0 qb2 qc1 qs2", "qc2 qa3 ro0 at1",
-    "qb3 qs3 pr0 qc3", "ro1 pr1 re0 at2", "at3 n20 gm00 gm01", "ro2 ga00 re1 ga01",
-    "ro3 gm02 ac00 pr2", "ga02 pr3 n21 ac01", "gm10 re2 ga10 ac02", "gm11 ga11 gm12 ac10",
-    "re3 n22 ga12 gm20", "ac11 ra00 n23 ga20", "dn00 ra10 gm21 ga21", "gm30 ra01 ga30 ra02",
-    "ac20 gm31 ga31 gm32", "ac21 dn10 ga32 ac12", "ra20 dn01 dn02 dn20", "ra11 ra21 fi0 ac30",
-    "dn11 ac31 ac32 ra12", "dn21 fi2 ra30 ou0", "dn12 fi1 ra31 dn30", "ra32 dn31 dn32 fi3",
-    "ou1 ou2 ou3",
+    "qa0 qb0 qa1 qx0", "qb1 qs1 qs0 qg0", "qa2 qc0 qb2 at0", "qs2 qg1 qa3 qc1",
+    "qg2 ro0 qb3 pr0", "at1 qc2 at2 ro1", "re0 qg3 qs3 pr1", "n20 gm00 gm01 ga00",
+    "ro2 qc3 re1 ga01", "gm02 at3 n21 ga02", "gm10 pr2 ac01 ro3", "ga10 gm11 pr3 re2",
+    "gm12 ra01 ga11 re3", "ac02 n22 ac00 ga12", "ac11 ac10 n23 gm20", "ga20 gm21 ra00 gm30",
+    "ac12 ra02 ga21 ga30", "ra10 gm31 ac20 dn00", "dn10 ac21 ra11 ga31", "dn11 dn01 gm32 ra20",
+    "dn02 ra21 ra12 ga32", "ac30 ac31 dn20 fi0", "ac32 dn21 ra30 dn12", "fi1 fi2 ra31 dn30",
+    "ra32 dn31 dn32 fi3", "ou2 ou1 ou0 ou3",
 )
 
 
@@ -110,15 +110,17 @@
 
     def d_copy(h, z, m=None, part=None):
         i = (h * 2 + z) * 3 + (0 if m is None else m)
-        src, dst = (d_send.at[pl.ds(i, 3)], d_recv.at[pl.ds(i, 3)]) if m is None else (d_send.at[i, part_rows(part)], d_recv.at[i, part_rows(part)])
-        k = 6 * NCH + m if part == 1 else i
+        sl = pl.ds(i, 3) if m is None else i
+        src, dst = (d_send.at[sl], d_recv.at[sl]) if part is None else (d_send.at[sl, part_rows(part)], d_recv.at[sl, part_rows(part)])
+        k = 6 * NCH if part == 1 else i
         return remote(src, dst, d_s.at[k], d_r.at[k], core_peer)
 
     def x_copy(h, m=None, part=None):
         i = h * 3 + (0 if m is None else m)
         k = h * 6 + (0 if m is None else m)
-        src, dst = (d_recv.at[pl.ds(k, 3)], x_recv.at[pl.ds(i, 3)]) if m is None else (d_recv.at[k, part_rows(part)], x_recv.at[i, part_rows(part)])
-        n = 3 * NCH + m if part == 1 else i
+        ssl, dsl = (pl.ds(k, 3), pl.ds(i, 3)) if m is None else (k, i)
+        src, dst = (d_recv.at[ssl], x_recv.at[dsl]) if part is None else (d_recv.at[ssl, part_rows(part)], x_recv.at[dsl, part_rows(part)])
+        n = 3 * NCH if part == 1 else i
         return remote(src, dst, x_s.at[n], x_r.at[n], x_peer)
 
     def o_copy(h, kind):
@@ -151,10 +153,11 @@
 
     def a_copy(h, j, kind):
         own = c * 2 + xc
-        slot = (own, own, c * 2 + 1 - xc)[kind]
+        direct = kind == 2 and piece(h, j)[1] < FW
+        slot = own if direct else (own, own, c * 2 + 1 - xc)[kind]
         i = (h * 4 + j) * 3 + kind
         ref = a_all.at[h, slot, :, pl.ds(*piece(h, j))]
-        return remote(ref, ref, a_s.at[i], a_r.at[i], (core_peer, x_peer, core_peer)[kind])
+        return remote(ref, ref, a_s.at[i], a_r.at[i], peer[3] if direct else (core_peer, x_peer, core_peer)[kind])
 
     def f_copy(h):
         return remote(f_send.at[h], f_recv.at[h], f_s.at[h], f_r.at[h], y_peer)
@@ -209,7 +212,7 @@
         n = ((x_own(h, s) - mean[sl]) * rstd[sl]).astype(BF)
         n_buf[h, pl.ds(pl.multiple_of(s * TOK, TOK), TOK)] = n
 
-    first_parts = [(m, part) for part in range(2) for m in range(3)]
+    first_parts = [(0, 0), (1, 0), (2, 0), (None, 1)]
 
     def norm_chunk(h):
         norm_rows(h, y, mean_o, rstd_o)
@@ -222,42 +225,37 @@
         d_copy(h, z).start()
 
     def qkv_take(h, z):
-        own = [dot(n_buf[h], wbuf[(2 - 2 * z) * 3 + m]) for m in range(3)]
         d_copy(h, z).wait_recv()
         for m in range(3):
             i = (h * 2 + z) * 3 + m
-            d_recv[i] = (own[m] + d_recv[i].astype(F32)).astype(BF)
-
-    def qkv_part(part):
-        rows = part_rows(part)
-
-        def give(m, carry):
-            if part == 0:
-                qkv_wait(3, m)
-            d_send[m, rows] = dot(n_buf[0, rows], wbuf[9 + m]).astype(BF)
-            d_copy(0, 0, m, part).start()
-            return carry
-
-        def take(m, carry):
-            if part == 0:
-                qkv_wait(2, m)
-            own = dot(n_buf[0, rows], wbuf[6 + m])
-            d_copy(0, 0, m, part).wait_recv()
-            d_recv[m, rows] = (own + d_recv[m, rows].astype(F32)).astype(BF)
-            x_copy(0, m, part).start()
-            return carry
-
-        lax.fori_loop(0, 3, give, 0)
-        lax.fori_loop(0, 3, take, 0)
+            d_recv[i] = (dot(n_buf[h], wbuf[(2 - 2 * z) * 3 + m]) + d_recv[i].astype(F32)).astype(BF)
 
     def step_qa(h, _):
         if h > 0:
             norm_chunk(h)
             qkv_give(h, 0)
-            qkv_give(h, 1)
-        else:
-            norm_rows(0, y, mean_o, rstd_o)
-            qkv_part(0)
+            return
+        norm_rows(0, y, mean_o, rstd_o)
+        rows = part_rows(0)
+
+        def give(m):
+            qkv_wait(3, m)
+            d_send[m, rows] = dot(n_buf[0, rows], wbuf[9 + m]).astype(BF)
+            d_copy(0, 0, m, 0).start()
+
+        def take(m):
+            qkv_wait(2, m)
+            own = dot(n_buf[0, rows], wbuf[6 + m])
+            d_copy(0, 0, m, 0).wait_recv()
+            d_recv[m, rows] = (own + d_recv[m, rows].astype(F32)).astype(BF)
+            x_copy(0, m, 0).start()
+
+        give(0)
+        give(1)
+        take(0)
+        give(2)
+        take(1)
+        take(2)
 
     def step_qb(h, _):
         if h > 0:
@@ -268,10 +266,23 @@
         other_moments.extend(moments((st1[4] + st1[5]) + (st1[6] + st1[7])))
         xy_copy(0).wait_recv()
         norm_rows(0, 1 - y, *other_moments)
-        qkv_part(1)
+        rows = part_rows(1)
         for m in range(3):
-            qkv_wait(1, m)
-        qkv_give(0, 1)
+            d_send[m, rows] = dot(n_buf[0, rows], wbuf[9 + m]).astype(BF)
+        d_copy(0, 0, None, 1).start()
+
+    def step_qx(h, _):
+        rows = part_rows(1)
+        d_copy(0, 0, None, 1).wait_recv()
+        for m in range(3):
+            d_recv[m, rows] = (dot(n_buf[0, rows], wbuf[6 + m]) + d_recv[m, rows].astype(F32)).astype(BF)
+        x_copy(0, None, 1).start()
+
+    def step_qg(h, _):
+        if h == 0:
+            for m in range(3):
+                qkv_wait(1, m)
+        qkv_give(h, 1)
 
     def step_qs(h, _):
         if h > 0:
@@ -373,9 +384,10 @@
     def steps(h, j, body):
         start, w = piece(h, j)
         lo, n = start // FW, w // FW
-        if n == 1:
-            body(lo, FW)
-        elif n > 1:
+        if n <= 2:
+            for kb in range(lo, lo + n):
+                body(kb, FW)
+        else:
             def step(kb, carry):
                 body(kb, FW)
                 return carry
@@ -428,11 +440,14 @@
         ]
         a_all[h, c * 2 + xc, :, cl] = (g * (1.0 / (1.0 + jnp.exp(-g))) * u).astype(BF)
         a_copy(h, j, 1).start()
+        if w < FW:
+            a_copy(h, j, 2).start()
         a_copy(h, j, 0).start()
 
     def step_ra(h, j):
         a_copy(h, j, 1).wait_recv()
-        a_copy(h, j, 2).start()
+        if piece(h, j)[1] >= FW:
+            a_copy(h, j, 2).start()
 
     def step_dn(h, j):
         if first_time("down"):
@@ -477,7 +492,7 @@
             own_slot[h, j] = free.pop(0)
         if name == "ga":
             free.append(own_slot[h, j])
-    step_of = dict(qa=step_qa, qb=step_qb, qs=step_qs, qc=step_qc, at=step_at, ro=step_ro, pr=step_pr, re=step_re, n2=step_n2,
+    step_of = dict(qa=step_qa, qb=step_qb, qx=step_qx, qg=step_qg, qs=step_qs, qc=step_qc, at=step_at, ro=step_ro, pr=step_pr, re=step_re, n2=step_n2,
                    gm=step_gm, ga=step_ga, ac=step_ac, ra=step_ra, dn=step_dn, fi=step_fi, ou=step_ou)
     for name, h, j in program:
         step_of[name](h, j)
@@ -550,7 +565,7 @@
                 vm((8, 2, 128), F32),
                 vm((NCH, 4, 2, 128), F32),
                 dma((NCH + 2,)), dma((48,)),
-                *(dma((n,)) for n in (NCH, 8, 6 * NCH + 3, 3 * NCH + 3, 3 * NCH, 2 * NCH, 4 * NCH, 4 * NCH, 4 * NCH, 12 * NCH, NCH) for _ in range(2)),
+                *(dma((n,)) for n in (NCH, 8, 6 * NCH + 1, 3 * NCH + 1, 3 * NCH, 2 * NCH, 4 * NCH, 4 * NCH, 4 * NCH, 12 * NCH, NCH) for _ in range(2)),
             ],
             compiler_params=pltpu.CompilerParams(collective_id=0, has_side_effects=True, vmem_limit_bytes=66256896),
             name="layer",

time: 95.7 us -> 95.2 us (level)
  no operation moved by 1% of the time
where the time goes in v8:
time: 95.2 us; the launch traced here: 95.1 us
  Pallas kernels  94.4 us (99%)
    pallas_call x1, Pallas kernels, layer_fn(): pl.pallas_call(layer_kernel, out_shape=pltpu.VMEM(x_blk.shape, BF), in_sp...  94.4 us

profile of v8, /device:TPU:0, one launch (start us, length us, event | category | flops | bytes accessed | tf_op | source)
XLA Modules:
  0.0 95.1 jit_solution(15819760559164980739)
XLA Ops:
  0.0 94.4 %layer.1 = bf16[1,128,1024]{2,1,0:T(8,128)(2,1)S(1)} custom-call(bf16[1,128,1024]{2,1,0:T(8,128)(2,1)} %x_hbm.1, bf16[1024,2048]{1,0:T(8,128)(2,1)} %wq_hbm.1, bf16[1024,2048]{1,0:T(8,128)(2,1)} %wk_hbm.1, bf16[1024,2048]{1,0:T(8,128)(2,1)} %wv_hbm.1, bf16[2048,1024]{1,0:T(8,128)(2,1)} %wo_hbm.1, bf16[1024,5504]{1,0:T(8,128)(2,1)} %wg_hbm.1, ...), custom_call_target="tpu_custom_call" | custom-call | tf_op jit(solution)/shard_map/layer/pallas_call | solution.py:534
  94.4 0.7 copy.12

commit v9 on v8

--- a/solution.py
+++ b/solution.py
@@ -384,7 +384,7 @@
     def steps(h, j, body):
         start, w = piece(h, j)
         lo, n = start // FW, w // FW
-        if n <= 2:
+        if n <= 1:
             for kb in range(lo, lo + n):
                 body(kb, FW)
         else:

time: 95.2 us -> 95.7 us (level)
  no operation moved by 1% of the time
where the time goes in v9:
time: 95.7 us; the launch traced here: 95.6 us
  Pallas kernels  94.9 us (99%)
    pallas_call x1, Pallas kernels, layer_fn(): pl.pallas_call(layer_kernel, out_shape=pltpu.VMEM(x_blk.shape, BF), in_sp...  94.9 us

profile of v9, /device:TPU:0, one launch (start us, length us, event | category | flops | bytes accessed | tf_op | source)
XLA Modules:
  0.0 95.6 jit_solution(8078434664765087684)
XLA Ops:
  0.0 94.9 %layer.1 = bf16[1,128,1024]{2,1,0:T(8,128)(2,1)S(1)} custom-call(bf16[1,128,1024]{2,1,0:T(8,128)(2,1)} %x_hbm.1, bf16[1024,2048]{1,0:T(8,128)(2,1)} %wq_hbm.1, bf16[1024,2048]{1,0:T(8,128)(2,1)} %wk_hbm.1, bf16[1024,2048]{1,0:T(8,128)(2,1)} %wv_hbm.1, bf16[2048,1024]{1,0:T(8,128)(2,1)} %wo_hbm.1, bf16[1024,5504]{1,0:T(8,128)(2,1)} %wg_hbm.1, ...), custom_call_target="tpu_custom_call" | custom-call | tf_op jit(solution)/shard_map/layer/pallas_call | solution.py:534
  94.9 0.7 copy.12

commit v10 on v9

--- a/solution.py
+++ b/solution.py
@@ -384,7 +384,7 @@
     def steps(h, j, body):
         start, w = piece(h, j)
         lo, n = start // FW, w // FW
-        if n <= 1:
+        if n <= 3:
             for kb in range(lo, lo + n):
                 body(kb, FW)
         else:

time: 95.7 us -> 95.2 us (level)
  no operation moved by 1% of the time
where the time goes in v10:
time: 95.2 us
  Pallas kernels  94.4 us (99%)
    pallas_call x1, Pallas kernels, layer_fn(): pl.pallas_call(layer_kernel, out_shape=pltpu.VMEM(x_blk.shape, BF), in_sp...  94.4 us

profile of v10, /device:TPU:0, one launch (start us, length us, event | category | flops | bytes accessed | tf_op | source)
XLA Modules:
  0.0 95.2 jit_solution(3819406964710276291)
XLA Ops:
  0.0 94.4 %layer.1 = bf16[1,128,1024]{2,1,0:T(8,128)(2,1)S(1)} custom-call(bf16[1,128,1024]{2,1,0:T(8,128)(2,1)} %x_hbm.1, bf16[1024,2048]{1,0:T(8,128)(2,1)} %wq_hbm.1, bf16[1024,2048]{1,0:T(8,128)(2,1)} %wk_hbm.1, bf16[1024,2048]{1,0:T(8,128)(2,1)} %wv_hbm.1, bf16[2048,1024]{1,0:T(8,128)(2,1)} %wo_hbm.1, bf16[1024,5504]{1,0:T(8,128)(2,1)} %wg_hbm.1, ...), custom_call_target="tpu_custom_call" | custom-call | tf_op jit(solution)/shard_map/layer/pallas_call | solution.py:534
  94.5 0.7 copy.12
